TPU v7x, 16 devices: a 4x2x1 block of a 4x4x8 slice. The times are simulated.
16 devices in a mesh: dp: 2 (over y, z), tp: 8 (over x, core).
Axes of the slice: x: 4, y: 2, z: 1, core: 2. Of those that a mesh axis runs over, the one named last changes fastest.
The devices are a block of a 4x4x8 slice.
Arguments:
- x_steps: bfloat16 [32, 128, 2048], P(None, 'dp'), parts along dimension 1
- cur_len: int32 [128], P('dp'), parts along dimension 0
- k_cache: bfloat16 [2, 128, 128, 16, 128], P(None, 'dp', None, 'tp'), parts along dimension 1
- v_cache: bfloat16 [2, 128, 128, 16, 128], P(None, 'dp', None, 'tp'), parts along dimension 1
- ln_gain: bfloat16 [2, 2048], replicated
- ln_bias: bfloat16 [2, 2048], replicated
- w_q: bfloat16 [2, 2048, 2048], P(None, None, 'tp')
- w_k: bfloat16 [2, 2048, 2048], P(None, None, 'tp')
- w_v: bfloat16 [2, 2048, 2048], P(None, None, 'tp')
- w_o: bfloat16 [2, 2048, 2048], P(None, 'tp')
- w_in: bfloat16 [2, 2048, 8192], P(None, None, 'tp')
- b_in: bfloat16 [2, 8192], P(None, 'tp')
- w_out: bfloat16 [2, 8192, 2048], P(None, 'tp')
- b_out: bfloat16 [2, 2048], replicated
Outputs:
- output 1: bfloat16 [32, 128, 2048], P(None, 'dp'), parts along dimension 1
- output 2: bfloat16 [2, 128, 128, 16, 128], P(None, 'dp', None, 'tp'), parts along dimension 1
- output 3: bfloat16 [2, 128, 128, 16, 128], P(None, 'dp', None, 'tp'), parts along dimension 1
There are 2 independent parts. A program takes and returns all parts, laid end to end along the dimension named above; an argument that names none is the same for every part.
All inputs are finite; a program needn't handle non-finite values.
Results may differ from a plain program's by a relative error of at most 0.0169117.
Values are sent between devices in bfloat16 or wider.
A program may use at most 768 MiB of HBM per device.

v0:
```python
import jax
import jax.numpy as jnp
from jax import lax
from jax.sharding import PartitionSpec as P

ROT_DIM = 64
LN_EPS = 1e-5


def layer_norm(hidden, gain, bias):
    hid_f32 = hidden.astype(jnp.float32)
    row_mean = jnp.mean(hid_f32, axis=-1, keepdims=True)
    centered = hid_f32 - row_mean
    row_var = jnp.mean(centered * centered, axis=-1, keepdims=True)
    normed = centered * lax.rsqrt(row_var + LN_EPS)
    return (normed * gain.astype(jnp.float32) + bias.astype(jnp.float32)).astype(jnp.bfloat16)


def rotary_tables(positions):
    inv_freq = 1.0 / (10000.0 ** (jnp.arange(0, ROT_DIM, 2).astype(jnp.float32) / ROT_DIM))
    angles = positions.astype(jnp.float32)[:, None] * inv_freq[None, :]
    return jnp.cos(angles)[:, None, :], jnp.sin(angles)[:, None, :]


def apply_rotary(vectors, cos_tab, sin_tab):
    lead_shape = vectors.shape[:-1]
    pairs = vectors[..., :ROT_DIM].reshape(lead_shape + (ROT_DIM // 2, 2))
    even_part = pairs[..., 0]
    odd_part = pairs[..., 1]
    rotated = jnp.stack([even_part * cos_tab - odd_part * sin_tab, odd_part * cos_tab + even_part * sin_tab], axis=-1)
    return jnp.concatenate([rotated.reshape(lead_shape + (ROT_DIM,)), vectors[..., ROT_DIM:]], axis=-1)


def attend(query, k_layer, v_layer, visible):
    score_scale = k_layer.shape[-1] ** -0.5
    scores = jnp.einsum("bhe,bshe->bhs", query, k_layer, preferred_element_type=jnp.float32) * score_scale
    scores = jnp.where(visible, scores, -jnp.inf)
    exp_scores = jnp.exp(scores - jnp.max(scores, axis=-1, keepdims=True))
    attn_probs = (exp_scores / jnp.sum(exp_scores, axis=-1, keepdims=True)).astype(jnp.bfloat16)
    context = jnp.einsum("bhs,bshe->bhe", attn_probs, v_layer, preferred_element_type=jnp.float32)
    return context.astype(jnp.bfloat16)


def step_setup(cur_len, step_idx, cache_len):
    new_pos = cur_len + step_idx
    slot_ids = jnp.arange(cache_len)
    visible = (slot_ids[None, :] <= new_pos[:, None])[:, None, :]
    return new_pos, rotary_tables(new_pos), visible


def layer_update(normed, new_pos, rotary, visible, caches, layer_idx, weights):
    cos_tab, sin_tab = rotary
    k_cache, v_cache = caches
    q_weight, k_weight, v_weight, o_weight, in_weight, in_bias, out_weight = weights
    batch = normed.shape[0]
    n_heads = k_cache.shape[3]
    head_dim = k_cache.shape[4]
    head_shape = (batch, n_heads, head_dim)
    query = jnp.dot(normed, q_weight, preferred_element_type=jnp.float32).reshape(head_shape)
    key_new = jnp.dot(normed, k_weight, preferred_element_type=jnp.float32).reshape(head_shape)
    value_new = jnp.dot(normed, v_weight, preferred_element_type=jnp.float32).astype(jnp.bfloat16).reshape(head_shape)
    query = apply_rotary(query, cos_tab, sin_tab).astype(jnp.bfloat16)
    key_new = apply_rotary(key_new, cos_tab, sin_tab).astype(jnp.bfloat16)
    batch_rows = jnp.arange(batch)
    k_cache = k_cache.at[layer_idx, batch_rows, new_pos].set(key_new)
    v_cache = v_cache.at[layer_idx, batch_rows, new_pos].set(value_new)
    context = attend(query, k_cache[layer_idx], v_cache[layer_idx], visible).reshape(batch, n_heads * head_dim)
    pre_act = jnp.dot(normed, in_weight, preferred_element_type=jnp.float32) + in_bias.astype(jnp.float32)
    gelu_act = jax.nn.gelu(pre_act, approximate=True).astype(jnp.bfloat16)
    layer_part = jnp.dot(context, o_weight, preferred_element_type=jnp.float32) + jnp.dot(gelu_act, out_weight, preferred_element_type=jnp.float32)
    return layer_part, k_cache, v_cache


def decode_shard(x_steps, cur_len, k_cache, v_cache, ln_gain, ln_bias, w_q, w_k, w_v, w_o, w_in, b_in, w_out, b_out):
    n_layers = k_cache.shape[0]
    outputs = []
    for step_idx in range(x_steps.shape[0]):
        new_pos, rotary, visible = step_setup(cur_len, step_idx, k_cache.shape[2])
        hidden = x_steps[step_idx]
        for layer_idx in range(n_layers):
            normed = layer_norm(hidden, ln_gain[layer_idx], ln_bias[layer_idx])
            weights = (w_q[layer_idx], w_k[layer_idx], w_v[layer_idx], w_o[layer_idx], w_in[layer_idx], b_in[layer_idx], w_out[layer_idx])
            layer_part, k_cache, v_cache = layer_update(normed, new_pos, rotary, visible, (k_cache, v_cache), layer_idx, weights)
            layer_sum = lax.psum(layer_part.astype(jnp.bfloat16), "tp")
            hidden = (hidden.astype(jnp.float32) + layer_sum.astype(jnp.float32) + b_out[layer_idx].astype(jnp.float32)).astype(jnp.bfloat16)
        outputs.append(hidden)
    return jnp.stack(outputs), k_cache, v_cache


def solution(mesh):
    cache_spec = P(None, "dp", None, "tp", None)
    in_specs = (P(None, "dp", None), P("dp"), cache_spec, cache_spec, P(None, None), P(None, None),
                P(None, None, "tp"), P(None, None, "tp"), P(None, None, "tp"), P(None, "tp", None),
                P(None, None, "tp"), P(None, "tp"), P(None, "tp", None), P(None, None))
    out_specs = (P(None, "dp", None), cache_spec, cache_spec)
    return jax.shard_map(decode_shard, mesh=mesh, in_specs=in_specs, out_specs=out_specs, check_vma=False)
```

profile of v0, /device:TPU:113, one launch (start us, length us, event | category | flops | bytes accessed | tf_op | source)
XLA Modules:
  0.0 5942.2 jit_solution(16064453841855778662)
XLA Ops:
  879.8 10.4 slice_bitcast_fusion.124
  929.5 10.4 slice_bitcast_fusion.122
  962.7 46.8 all-reduce.37.cloned.1.call-done
  1093.9 10.4 slice_bitcast_fusion.118
  1125.5 45.1 all-reduce.39.cloned.1.call-done
  1253.8 10.6 slice_bitcast_fusion.114
  1284.9 45.1 all-reduce.41.cloned.1.call-done
  1413.3 10.6 slice_bitcast_fusion.110
  1444.4 45.1 all-reduce.43.cloned.1.call-done
  1572.8 10.6 slice_bitcast_fusion.106
  1603.9 45.1 all-reduce.45.cloned.1.call-done
  1731.6 10.6 slice_bitcast_fusion.102
  1762.6 45.1 all-reduce.47.cloned.1.call-done
  1890.3 10.6 slice_bitcast_fusion.98
  1920.6 45.1 all-reduce.49.cloned.1.call-done
  2049.0 10.6 slice_bitcast_fusion.94
  2079.3 45.1 all-reduce.51.cloned.1.call-done
  2207.7 10.6 slice_bitcast_fusion.90
  2238.0 45.2 all-reduce.53.cloned.1.call-done
  2366.4 10.6 slice_bitcast_fusion.86
  2396.8 45.1 all-reduce.55.cloned.1.call-done
  2525.1 10.6 slice_bitcast_fusion.82
  2555.4 45.1 all-reduce.57.cloned.1.call-done
  2683.8 10.6 slice_bitcast_fusion.78
  2714.1 45.2 all-reduce.59.cloned.1.call-done
  2842.6 10.6 slice_bitcast_fusion.74
  2872.8 45.2 all-reduce.61.cloned.1.call-done
  3001.2 10.6 slice_bitcast_fusion.70
  3031.5 45.1 all-reduce.63.cloned.1.call-done
  3159.9 10.6 slice_bitcast_fusion.66
  3190.3 45.1 all-reduce.65.cloned.1.call-done
  3318.7 10.6 slice_bitcast_fusion.62
  3348.9 45.1 all-reduce.67.cloned.1.call-done
  3477.3 10.6 slice_bitcast_fusion.58
  3507.6 45.1 all-reduce.69.cloned.1.call-done
  3636.0 10.6 slice_bitcast_fusion.54
  3666.3 45.2 all-reduce.71.cloned.1.call-done
  3794.7 10.6 slice_bitcast_fusion.50
  3825.1 45.1 all-reduce.73.cloned.1.call-done
  3953.4 10.6 slice_bitcast_fusion.46
  3983.8 45.1 all-reduce.75.cloned.1.call-done
  4112.2 10.6 slice_bitcast_fusion.42
  4142.5 45.1 all-reduce.77.cloned.1.call-done
  4270.9 10.6 slice_bitcast_fusion.38
  4301.2 45.1 all-reduce.79.cloned.1.call-done
  4429.6 10.6 slice_bitcast_fusion.34
  4459.9 45.1 all-reduce.81.cloned.1.call-done
  4588.4 10.6 slice_bitcast_fusion.30
  4618.7 45.1 all-reduce.83.cloned.1.call-done
  4747.1 10.6 slice_bitcast_fusion.26
  4777.4 45.2 all-reduce.85.cloned.1.call-done
  4905.8 10.6 slice_bitcast_fusion.22
  4936.1 45.2 all-reduce.87.cloned.1.call-done
  5064.5 10.6 slice_bitcast_fusion.18
  5094.9 45.2 all-reduce.89.cloned.1.call-done
  5223.3 10.6 slice_bitcast_fusion.14
  5253.6 45.1 all-reduce.91.cloned.1.call-done
  5382.0 10.6 slice_bitcast_fusion.10
  5412.3 45.1 all-reduce.93.cloned.1.call-done
  5540.8 10.6 slice_bitcast_fusion.6
  5571.1 45.1 all-reduce.95.cloned.1.call-done
  5699.5 10.6 slice_bitcast_fusion.2
  5729.8 45.1 all-reduce.97.cloned.1.call-done
  5822.7 98.4 %all-reduce.99.cloned.1.call-done = (bf16[64,2048]{1,0:T(8,128)(2,1)}, bf16[64,2048]{1,0:T(8,128)(2,1)}, bf16[64,2048]{1,0:T(8,128)(2,1)}, bf16[64,2048]{1,0:T(8...) async-done(((bf16[64,2048]{1,0:T(8,128)(2,1)}, ...) | async-done | bytes 8388624 | tf_op jit(solution)/shard_map/psum | solution.py:84
  (3109 shorter events, 4080.7 us)
Async XLA Ops:
  7.2 831.0 %all-reduce.35.cloned.1.call-start = ((), (), s32[]{:S(2)}) async-start(), calls=%async_computation | async-start | bytes 524288 | tf_op jit(solution)/shard_map/psum | solution.py:84
  40.2 597.6 %copy-start.249 = (f32[64,32]{0,1:T(8,128)}, f32[64,32]{0,1:T(8,128)S(1)}, u32[]{:S(2)}) copy-start(f32[64,32]{0,1:T(8,128)S(1)} %get-tuple-element.806) | copy-start | bytes 24580
  40.2 602.5 %copy-start.245 = (f32[64,32]{0,1:T(8,128)}, f32[64,32]{0,1:T(8,128)S(1)}, u32[]{:S(2)}) copy-start(f32[64,32]{0,1:T(8,128)S(1)} %get-tuple-element.561) | copy-start | bytes 24580
  40.2 602.5 %copy-start.247 = (f32[64,32]{0,1:T(8,128)}, f32[64,32]{0,1:T(8,128)S(1)}, u32[]{:S(2)}) copy-start(f32[64,32]{0,1:T(8,128)S(1)} %get-tuple-element.562) | copy-start | bytes 24580
  95.9 913.7 %all-reduce.37.cloned.1.call-start = ((), (), s32[]{:S(2)}) async-start(), calls=%async_computation.1 | async-start | bytes 524288 | tf_op jit(solution)/shard_map/psum | solution.py:84
  100.1 154.7 %copy-start.522 = (f32[64]{0:T(128)}, f32[64]{0:T(128)S(1)}, u32[]{:S(2)}) copy-start(f32[64]{0:T(128)S(1)} %get-tuple-element.864) | copy-start | bytes 772
  100.1 156.4 %copy-start.524 = (f32[64]{0:T(128)}, f32[64]{0:T(128)S(1)}, u32[]{:S(2)}) copy-start(f32[64]{0:T(128)S(1)} %get-tuple-element.865) | copy-start | bytes 772
  100.1 151.2 %copy-start.518 = (f32[64]{0:T(128)}, f32[64]{0:T(128)S(1)}, u32[]{:S(2)}) copy-start(f32[64]{0:T(128)S(1)} %get-tuple-element.862) | copy-start | bytes 772
  100.1 152.9 %copy-start.520 = (f32[64]{0:T(128)}, f32[64]{0:T(128)S(1)}, u32[]{:S(2)}) copy-start(f32[64]{0:T(128)S(1)} %get-tuple-element.863) | copy-start | bytes 772
  100.1 147.9 %copy-start.514 = (f32[64]{0:T(128)}, f32[64]{0:T(128)S(1)}, u32[]{:S(2)}) copy-start(f32[64]{0:T(128)S(1)} %get-tuple-element.860) | copy-start | bytes 772
  100.1 149.5 %copy-start.516 = (f32[64]{0:T(128)}, f32[64]{0:T(128)S(1)}, u32[]{:S(2)}) copy-start(f32[64]{0:T(128)S(1)} %get-tuple-element.861) | copy-start | bytes 772
  100.2 144.4 %copy-start.510 = (f32[64]{0:T(128)}, f32[64]{0:T(128)S(1)}, u32[]{:S(2)}) copy-start(f32[64]{0:T(128)S(1)} %get-tuple-element.858) | copy-start | bytes 772
  100.2 146.1 %copy-start.512 = (f32[64]{0:T(128)}, f32[64]{0:T(128)S(1)}, u32[]{:S(2)}) copy-start(f32[64]{0:T(128)S(1)} %get-tuple-element.859) | copy-start | bytes 772
  107.8 135.1 %copy-start.508 = (f32[64]{0:T(128)}, f32[64]{0:T(128)S(1)}, u32[]{:S(2)}) copy-start(f32[64]{0:T(128)S(1)} %get-tuple-element.856) | copy-start | bytes 772
  107.8 150.4 %copy-start.526 = (f32[64]{0:T(128)}, f32[64]{0:T(128)S(1)}, u32[]{:S(2)}) copy-start(f32[64]{0:T(128)S(1)} %get-tuple-element.857) | copy-start | bytes 772
  108.3 151.6 %copy-start.528 = (f32[64]{0:T(128)}, f32[64]{0:T(128)S(1)}, u32[]{:S(2)}) copy-start(f32[64]{0:T(128)S(1)} %get-tuple-element.866) | copy-start | bytes 772
  137.2 162.3 %copy-start.317 = (f32[64,2,128]{2,0,1:T(8,128)}, f32[64,2,128]{2,0,1:T(8,128)S(1)}, u32[]{:S(2)}) copy-start(f32[64,2,128]{2,0,1:T(8,128)S(1)} %fusion.3336) | copy-start | bytes 196612
  141.5 158.7 %copy-start.318 = (f32[64,2,128]{2,0,1:T(8,128)}, f32[64,2,128]{2,0,1:T(8,128)S(1)}, u32[]{:S(2)}) copy-start(f32[64,2,128]{2,0,1:T(8,128)S(1)} %fusion.3347) | copy-start | bytes 196612
  145.8 155.2 %copy-start.319 = (f32[64,2,128]{2,0,1:T(8,128)}, f32[64,2,128]{2,0,1:T(8,128)S(1)}, u32[]{:S(2)}) copy-start(f32[64,2,128]{2,0,1:T(8,128)S(1)} %fusion.3358) | copy-start | bytes 196612
  150.0 151.7 %copy-start.320 = (f32[64,2,128]{2,0,1:T(8,128)}, f32[64,2,128]{2,0,1:T(8,128)S(1)}, u32[]{:S(2)}) copy-start(f32[64,2,128]{2,0,1:T(8,128)S(1)} %fusion.3369) | copy-start | bytes 196612
  154.2 148.1 %copy-start.321 = (f32[64,2,128]{2,0,1:T(8,128)}, f32[64,2,128]{2,0,1:T(8,128)S(1)}, u32[]{:S(2)}) copy-start(f32[64,2,128]{2,0,1:T(8,128)S(1)} %fusion.3380) | copy-start | bytes 196612
  158.5 144.5 %copy-start.322 = (f32[64,2,128]{2,0,1:T(8,128)}, f32[64,2,128]{2,0,1:T(8,128)S(1)}, u32[]{:S(2)}) copy-start(f32[64,2,128]{2,0,1:T(8,128)S(1)} %fusion.3391) | copy-start | bytes 196612
  162.8 140.9 %copy-start.323 = (f32[64,2,128]{2,0,1:T(8,128)}, f32[64,2,128]{2,0,1:T(8,128)S(1)}, u32[]{:S(2)}) copy-start(f32[64,2,128]{2,0,1:T(8,128)S(1)} %fusion.3402) | copy-start | bytes 196612
  167.2 137.1 %copy-start.324 = (f32[64,2,128]{2,0,1:T(8,128)}, f32[64,2,128]{2,0,1:T(8,128)S(1)}, u32[]{:S(2)}) copy-start(f32[64,2,128]{2,0,1:T(8,128)S(1)} %fusion.3413) | copy-start | bytes 196612
  171.5 133.5 %copy-start.325 = (f32[64,2,128]{2,0,1:T(8,128)}, f32[64,2,128]{2,0,1:T(8,128)S(1)}, u32[]{:S(2)}) copy-start(f32[64,2,128]{2,0,1:T(8,128)S(1)} %fusion.3424) | copy-start | bytes 196612
  176.0 129.7 %copy-start.326 = (f32[64,2,128]{2,0,1:T(8,128)}, f32[64,2,128]{2,0,1:T(8,128)S(1)}, u32[]{:S(2)}) copy-start(f32[64,2,128]{2,0,1:T(8,128)S(1)} %fusion.3435) | copy-start | bytes 196612
  180.3 126.1 %copy-start.327 = (f32[64,2,128]{2,0,1:T(8,128)}, f32[64,2,128]{2,0,1:T(8,128)S(1)}, u32[]{:S(2)}) copy-start(f32[64,2,128]{2,0,1:T(8,128)S(1)} %fusion.3446) | copy-start | bytes 196612
  184.5 122.5 %copy-start.328 = (f32[64,2,128]{2,0,1:T(8,128)}, f32[64,2,128]{2,0,1:T(8,128)S(1)}, u32[]{:S(2)}) copy-start(f32[64,2,128]{2,0,1:T(8,128)S(1)} %fusion.3457) | copy-start | bytes 196612
  193.6 114.2 %copy-start.329 = (f32[64,2,128]{2,0,1:T(8,128)}, f32[64,2,128]{2,0,1:T(8,128)S(1)}, u32[]{:S(2)}) copy-start(f32[64,2,128]{2,0,1:T(8,128)S(1)} %fusion.3468) | copy-start | bytes 196612
  197.8 110.6 %copy-start.330 = (f32[64,2,128]{2,0,1:T(8,128)}, f32[64,2,128]{2,0,1:T(8,128)S(1)}, u32[]{:S(2)}) copy-start(f32[64,2,128]{2,0,1:T(8,128)S(1)} %fusion.3479) | copy-start | bytes 196612
  637.8 110.0 %copy-start.316 = (f32[64,2,128]{2,0,1:T(8,128)S(1)}, f32[64,2,128]{2,0,1:T(8,128)}, u32[]{:S(2)}) copy-start(f32[64,2,128]{2,0,1:T(8,128)} %fusion.3270) | copy-start | bytes 196612
  839.4 117.3 %copy-start.89 = (bf16[64,2048]{1,0:T(8,128)(2,1)}, bf16[64,2048]{1,0:T(8,128)(2,1)S(1)}, u32[]{:S(2)}) copy-start(bf16[64,2048]{1,0:T(8,128)(2,1)S(1)} %get-tuple-element.162) | copy-start | bytes 786436
  956.6 214.0 %all-reduce.39.cloned.1.call-start = ((), (), s32[]{:S(2)}) async-start(), calls=%async_computation.2 | async-start | bytes 524288 | tf_op jit(solution)/shard_map/psum | solution.py:84
  1010.8 108.8 %copy-start.91 = (bf16[64,2048]{1,0:T(8,128)(2,1)}, bf16[64,2048]{1,0:T(8,128)(2,1)S(1)}, u32[]{:S(2)}) copy-start(bf16[64,2048]{1,0:T(8,128)(2,1)S(1)} %get-tuple-element.160) | copy-start | bytes 786436
  1119.5 210.5 %all-reduce.41.cloned.1.call-start = ((), (), s32[]{:S(2)}) async-start(), calls=%async_computation.3 | async-start | bytes 524288 | tf_op jit(solution)/shard_map/psum | solution.py:84
  1278.9 210.6 %all-reduce.43.cloned.1.call-start = ((), (), s32[]{:S(2)}) async-start(), calls=%async_computation.4 | async-start | bytes 524288 | tf_op jit(solution)/shard_map/psum | solution.py:84
  1438.4 210.6 %all-reduce.45.cloned.1.call-start = ((), (), s32[]{:S(2)}) async-start(), calls=%async_computation.5 | async-start | bytes 524288 | tf_op jit(solution)/shard_map/psum | solution.py:84
  1597.9 209.8 %all-reduce.47.cloned.1.call-start = ((), (), s32[]{:S(2)}) async-start(), calls=%async_computation.6 | async-start | bytes 524288 | tf_op jit(solution)/shard_map/psum | solution.py:84
  1756.6 209.1 %all-reduce.49.cloned.1.call-start = ((), (), s32[]{:S(2)}) async-start(), calls=%async_computation.7 | async-start | bytes 524288 | tf_op jit(solution)/shard_map/psum | solution.py:84
  1914.7 209.8 %all-reduce.51.cloned.1.call-start = ((), (), s32[]{:S(2)}) async-start(), calls=%async_computation.8 | async-start | bytes 524288 | tf_op jit(solution)/shard_map/psum | solution.py:84
  2073.4 209.8 %all-reduce.53.cloned.1.call-start = ((), (), s32[]{:S(2)}) async-start(), calls=%async_computation.9 | async-start | bytes 524288 | tf_op jit(solution)/shard_map/psum | solution.py:84
  2232.1 209.8 %all-reduce.55.cloned.1.call-start = ((), (), s32[]{:S(2)}) async-start(), calls=%async_computation.10 | async-start | bytes 524288 | tf_op jit(solution)/shard_map/psum | solution.py:84
  2390.8 209.8 %all-reduce.57.cloned.1.call-start = ((), (), s32[]{:S(2)}) async-start(), calls=%async_computation.11 | async-start | bytes 524288 | tf_op jit(solution)/shard_map/psum | solution.py:84
  2549.5 209.8 %all-reduce.59.cloned.1.call-start = ((), (), s32[]{:S(2)}) async-start(), calls=%async_computation.12 | async-start | bytes 524288 | tf_op jit(solution)/shard_map/psum | solution.py:84
  2708.2 209.8 %all-reduce.61.cloned.1.call-start = ((), (), s32[]{:S(2)}) async-start(), calls=%async_computation.13 | async-start | bytes 524288 | tf_op jit(solution)/shard_map/psum | solution.py:84
  2866.9 209.8 %all-reduce.63.cloned.1.call-start = ((), (), s32[]{:S(2)}) async-start(), calls=%async_computation.14 | async-start | bytes 524288 | tf_op jit(solution)/shard_map/psum | solution.py:84
  3025.6 209.8 %all-reduce.65.cloned.1.call-start = ((), (), s32[]{:S(2)}) async-start(), calls=%async_computation.15 | async-start | bytes 524288 | tf_op jit(solution)/shard_map/psum | solution.py:84
  3184.3 209.8 %all-reduce.67.cloned.1.call-start = ((), (), s32[]{:S(2)}) async-start(), calls=%async_computation.16 | async-start | bytes 524288 | tf_op jit(solution)/shard_map/psum | solution.py:84
  3343.0 209.8 %all-reduce.69.cloned.1.call-start = ((), (), s32[]{:S(2)}) async-start(), calls=%async_computation.17 | async-start | bytes 524288 | tf_op jit(solution)/shard_map/psum | solution.py:84
  3501.7 209.8 %all-reduce.71.cloned.1.call-start = ((), (), s32[]{:S(2)}) async-start(), calls=%async_computation.18 | async-start | bytes 524288 | tf_op jit(solution)/shard_map/psum | solution.py:84
  3660.4 209.8 %all-reduce.73.cloned.1.call-start = ((), (), s32[]{:S(2)}) async-start(), calls=%async_computation.19 | async-start | bytes 524288 | tf_op jit(solution)/shard_map/psum | solution.py:84
  3819.1 209.8 %all-reduce.75.cloned.1.call-start = ((), (), s32[]{:S(2)}) async-start(), calls=%async_computation.20 | async-start | bytes 524288 | tf_op jit(solution)/shard_map/psum | solution.py:84
  3977.8 209.8 %all-reduce.77.cloned.1.call-start = ((), (), s32[]{:S(2)}) async-start(), calls=%async_computation.21 | async-start | bytes 524288 | tf_op jit(solution)/shard_map/psum | solution.py:84
  4136.5 209.8 %all-reduce.79.cloned.1.call-start = ((), (), s32[]{:S(2)}) async-start(), calls=%async_computation.22 | async-start | bytes 524288 | tf_op jit(solution)/shard_map/psum | solution.py:84
  4295.3 209.8 %all-reduce.81.cloned.1.call-start = ((), (), s32[]{:S(2)}) async-start(), calls=%async_computation.23 | async-start | bytes 524288 | tf_op jit(solution)/shard_map/psum | solution.py:84
  4454.0 209.8 %all-reduce.83.cloned.1.call-start = ((), (), s32[]{:S(2)}) async-start(), calls=%async_computation.24 | async-start | bytes 524288 | tf_op jit(solution)/shard_map/psum | solution.py:84
  4612.8 209.8 %all-reduce.85.cloned.1.call-start = ((), (), s32[]{:S(2)}) async-start(), calls=%async_computation.25 | async-start | bytes 524288 | tf_op jit(solution)/shard_map/psum | solution.py:84
  4771.5 209.8 %all-reduce.87.cloned.1.call-start = ((), (), s32[]{:S(2)}) async-start(), calls=%async_computation.26 | async-start | bytes 524288 | tf_op jit(solution)/shard_map/psum | solution.py:84
  4930.2 209.9 %all-reduce.89.cloned.1.call-start = ((), (), s32[]{:S(2)}) async-start(), calls=%async_computation.27 | async-start | bytes 524288 | tf_op jit(solution)/shard_map/psum | solution.py:84
  5088.9 209.8 %all-reduce.91.cloned.1.call-start = ((), (), s32[]{:S(2)}) async-start(), calls=%async_computation.28 | async-start | bytes 524288 | tf_op jit(solution)/shard_map/psum | solution.py:84
  5247.6 209.8 %all-reduce.93.cloned.1.call-start = ((), (), s32[]{:S(2)}) async-start(), calls=%async_computation.29 | async-start | bytes 524288 | tf_op jit(solution)/shard_map/psum | solution.py:84
  5406.4 209.9 %all-reduce.95.cloned.1.call-start = ((), (), s32[]{:S(2)}) async-start(), calls=%async_computation.30 | async-start | bytes 524288 | tf_op jit(solution)/shard_map/psum | solution.py:84
  5565.1 209.8 %all-reduce.97.cloned.1.call-start = ((), (), s32[]{:S(2)}) async-start(), calls=%async_computation.31 | async-start | bytes 524288 | tf_op jit(solution)/shard_map/psum | solution.py:84
  5723.9 197.3 %all-reduce.99.cloned.1.call-start = ((), (), s32[]{:S(2)}) async-start(), calls=%async_computation.32 | async-start | bytes 16777216 | tf_op jit(solution)/shard_map/psum | solution.py:84
  (548 other events, 15309.0 us)
Sparse Core Ops, SparseCore 0:
  95.9 52.9 all-reduce.34
  956.7 52.7 all-reduce.36
  1119.6 50.9 all-reduce.38
  1279.1 50.9 all-reduce.40
  1438.6 50.9 all-reduce.42
  1598.0 50.9 all-reduce.44
  1756.8 50.9 all-reduce.46
  1914.8 50.9 all-reduce.48
  2073.5 50.9 all-reduce.50
  2232.2 50.9 all-reduce.52
  2390.9 50.9 all-reduce.54
  2549.6 50.9 all-reduce.56
  2708.3 50.9 all-reduce.58
  2867.0 50.9 all-reduce.60
  3025.7 50.9 all-reduce.62
  3184.4 50.9 all-reduce.64
  3343.1 50.9 all-reduce.66
  3501.8 50.9 all-reduce.68
  3660.5 50.9 all-reduce.70
  3819.2 50.9 all-reduce.72
  3977.9 50.9 all-reduce.74
  4136.7 50.9 all-reduce.76
  4295.4 50.9 all-reduce.78
  4454.1 50.9 all-reduce.80
  4612.9 50.9 all-reduce.82
  4771.6 50.9 all-reduce.84
  4930.3 50.9 all-reduce.86
  5089.1 50.9 all-reduce.88
  5247.8 50.9 all-reduce.90
  5406.5 50.9 all-reduce.92
  5565.3 50.9 all-reduce.94
  5724.0 50.9 all-reduce.96
  5822.8 98.3 all-reduce.98
where the time goes:
time: 5990 us; the launch traced here: 5940 us
  local copies, waits for them, and re-layouts  2840 us (47%)
  waiting for transfers between devices  1500 us (25%)
  matrix products  1170 us (20%)
  other arithmetic  397 us (7%)
    psum x33, waiting for transfers between devices, decode_shard(): layer_sum = lax.psum(layer_part.astype(jnp.bfloat16), 'tp')  1500 us
    squeeze x64, local copies, waits for them, and re-layouts, layer_update(): v_cache[layer_idx]  666 us
    squeeze x64, local copies, waits for them, and re-layouts, layer_update(): k_cache[layer_idx]  656 us
    scatter x64, local copies, waits for them, and re-layouts, layer_update(): k_cache = k_cache.at[layer_idx, batch_rows, new_pos].set(key_new)  581 us
    scatter x64, local copies, waits for them, and re-layouts, layer_update(): v_cache = v_cache.at[layer_idx, batch_rows, new_pos].set(value_new)  564 us
    dot_general x64, matrix products, layer_update(): jnp.dot(gelu_act, out_weight, preferred_element_type=jnp.float32)  381 us
    dot_general x64, matrix products, attend(): jnp.einsum('bhe,bshe->bhs', query, k_layer, preferred_element_type=jnp.fl...  222 us
    dot_general x64, matrix products, attend(): jnp.einsum('bhs,bshe->bhe', attn_probs, v_layer, preferred_element_type=j...  214 us
  transfers between devices with their start and end apart: 33, of which 32 were waited for; matrix products, arithmetic and copies ran while one was open for 16% of the time, Pallas kernels for 0%

commit v1 on v0

v1 whole, which is shorter than its diff:
```python
import jax
import jax.numpy as jnp
from jax import lax
from jax.sharding import PartitionSpec as P

ROT_DIM = 64
LN_EPS = 1e-5
N_CHUNKS = 4


def layer_norm(hidden, gain, bias):
    hid_f32 = hidden.astype(jnp.float32)
    row_mean = jnp.mean(hid_f32, axis=-1, keepdims=True)
    centered = hid_f32 - row_mean
    row_var = jnp.mean(centered * centered, axis=-1, keepdims=True)
    normed = centered * lax.rsqrt(row_var + LN_EPS)
    return (normed * gain.astype(jnp.float32) + bias.astype(jnp.float32)).astype(jnp.bfloat16)


def rotary_tables(positions):
    inv_freq = 1.0 / (10000.0 ** (jnp.arange(0, ROT_DIM, 2).astype(jnp.float32) / ROT_DIM))
    angles = positions.astype(jnp.float32)[..., None] * inv_freq
    return jnp.cos(angles)[:, :, None, :], jnp.sin(angles)[:, :, None, :]


def apply_rotary(vectors, cos_tab, sin_tab):
    lead_shape = vectors.shape[:-1]
    pairs = vectors[..., :ROT_DIM].reshape(lead_shape + (ROT_DIM // 2, 2))
    even_part = pairs[..., 0]
    odd_part = pairs[..., 1]
    rotated = jnp.stack([even_part * cos_tab - odd_part * sin_tab, odd_part * cos_tab + even_part * sin_tab], axis=-1)
    return jnp.concatenate([rotated.reshape(lead_shape + (ROT_DIM,)), vectors[..., ROT_DIM:]], axis=-1)


def layer_chunk(hidden, positions, k_old, v_old, gain, bias, weights):
    q_weight, k_weight, v_weight, o_weight, in_weight, in_bias, out_weight = weights
    steps, batch, _ = hidden.shape
    _, slots, heads, head_dim = k_old.shape
    normed = layer_norm(hidden, gain, bias)
    head_shape = (steps, batch, heads, head_dim)
    dot = lambda a, w: jnp.einsum("tbd,df->tbf", a, w, preferred_element_type=jnp.float32)
    rotary = rotary_tables(positions)
    query = apply_rotary(dot(normed, q_weight).reshape(head_shape), *rotary).astype(jnp.bfloat16)
    key_new = apply_rotary(dot(normed, k_weight).reshape(head_shape), *rotary).astype(jnp.bfloat16)
    value_new = dot(normed, v_weight).reshape(head_shape).astype(jnp.bfloat16)
    slot_ids = jnp.arange(slots)
    place = positions.T[:, None, :] == slot_ids[None, :, None]
    written = jnp.any(place, axis=-1)[:, :, None, None]
    onehot = place.astype(jnp.bfloat16)
    put = lambda new, old: jnp.where(
        written, jnp.einsum("bst,tbhe->bshe", onehot, new, preferred_element_type=jnp.float32).astype(jnp.bfloat16), old)
    k_all = put(key_new, k_old)
    v_all = put(value_new, v_old)
    scores = jnp.einsum("tbhe,bshe->bhts", query, k_all, preferred_element_type=jnp.float32) * (head_dim ** -0.5)
    visible = slot_ids[None, None, None, :] <= positions.T[:, None, :, None]
    scores = jnp.where(visible, scores, -jnp.inf)
    exp_scores = jnp.exp(scores - jnp.max(scores, axis=-1, keepdims=True))
    probs = (exp_scores / jnp.sum(exp_scores, axis=-1, keepdims=True)).astype(jnp.bfloat16)
    context = jnp.einsum("bhts,bshe->tbhe", probs, v_all, preferred_element_type=jnp.float32).astype(jnp.bfloat16)
    context = context.reshape(steps, batch, heads * head_dim)
    pre_act = dot(normed, in_weight) + in_bias.astype(jnp.float32)
    act = jax.nn.gelu(pre_act, approximate=True).astype(jnp.bfloat16)
    return dot(context, o_weight) + dot(act, out_weight), k_all, v_all


def decode_shard(x_steps, cur_len, k_cache, v_cache, ln_gain, ln_bias, w_q, w_k, w_v, w_o, w_in, b_in, w_out, b_out):
    steps, batch, _ = x_steps.shape
    n_layers = k_cache.shape[0]
    size = batch // N_CHUNKS
    positions = cur_len[None, :] + jnp.arange(steps)[:, None]
    hidden = [x_steps[:, c * size:(c + 1) * size] for c in range(N_CHUNKS)]
    k_layers, v_layers = [], []
    for layer in range(n_layers):
        weights = (w_q[layer], w_k[layer], w_v[layer], w_o[layer], w_in[layer], b_in[layer], w_out[layer])
        k_parts, v_parts = [], []
        for c in range(N_CHUNKS):
            rows = slice(c * size, (c + 1) * size)
            part, k_new, v_new = layer_chunk(hidden[c], positions[:, rows], k_cache[layer, rows], v_cache[layer, rows],
                                             ln_gain[layer], ln_bias[layer], weights)
            total = lax.psum(part.astype(jnp.bfloat16), "tp")
            hidden[c] = (hidden[c].astype(jnp.float32) + total.astype(jnp.float32)
                         + b_out[layer].astype(jnp.float32)).astype(jnp.bfloat16)
            k_parts.append(k_new)
            v_parts.append(v_new)
        k_layers.append(jnp.concatenate(k_parts))
        v_layers.append(jnp.concatenate(v_parts))
    return jnp.concatenate(hidden, axis=1), jnp.stack(k_layers), jnp.stack(v_layers)


def solution(mesh):
    cache_spec = P(None, "dp", None, "tp", None)
    in_specs = (P(None, "dp", None), P("dp"), cache_spec, cache_spec, P(None, None), P(None, None),
                P(None, None, "tp"), P(None, None, "tp"), P(None, None, "tp"), P(None, "tp", None),
                P(None, None, "tp"), P(None, "tp"), P(None, "tp", None), P(None, None))
    out_specs = (P(None, "dp", None), cache_spec, cache_spec)
    return jax.shard_map(decode_shard, mesh=mesh, in_specs=in_specs, out_specs=out_specs, check_vma=False)
```

time: 5990 us -> 670 us (0.11)
  local copies, waits for them, and re-layouts: 2840 us -> 147 us
  waiting for transfers between devices: 1500 us -> 129 us
  matrix products: 1170 us -> 247 us
  other arithmetic: 397 us -> 119 us
    psum x33 -> x2, waiting for transfers between devices: 1500 us -> 129 us  [decode_shard(): total = lax.psum(part.astype(jnp.bfloat16), 'tp')]
    squeeze x128 -> x0, local copies, waits for them, and re-layouts: 1320 us -> none  [the longest x64 666 us: layer_update(): v_cache[layer_idx]]
    scatter x128 -> x0, local copies, waits for them, and re-layouts: 1140 us -> none  [the longest x64 581 us: layer_update(): k_cache = k_cache.at[layer_idx, batch_rows, new_pos].set(key_new)]
    dot_general x448 -> x72, matrix products: 1170 us -> 247 us  [the longest x40 180 us: layer_chunk(): jnp.einsum('tbd,df->tbf', a, w, preferred_element_type=jnp.float32)]
    reshape x128 -> x16, local copies, waits for them, and re-layouts: 88.7 us -> 10.7 us  [apply_rotary(): rotated.reshape(lead_shape + (ROT_DIM,))]
    slice x128 -> x16, local copies, waits for them, and re-layouts: 94.5 us -> 26 us  [apply_rotary(): pairs = vectors[..., :ROT_DIM].reshape(lead_shape + (ROT_DIM // 2, 2))]
    concatenate x128 -> x16, other arithmetic: 85.4 us -> 17.8 us  [apply_rotary(): jnp.concatenate([rotated.reshape(lead_shape + (ROT_DIM,)), vectors[..., R...]
  transfers between devices with their start and end apart: 33 -> 2, of which waited for: 32 -> 2; matrix products, arithmetic and copies ran while one was open for 16% -> 9% of each run, Pallas kernels for 0% -> 0%
where the time goes in v1:
time: 670 us; the launch traced here: 658 us
  matrix products  247 us (37%)
  local copies, waits for them, and re-layouts  147 us (22%)
  waiting for transfers between devices  129 us (19%)
  other arithmetic  119 us (18%)
  between operations  15.9 us (2%)
    dot_general x40, matrix products, layer_chunk(): jnp.einsum('tbd,df->tbf', a, w, preferred_element_type=jnp.float32)  180 us
    psum x2, waiting for transfers between devices, decode_shard(): total = lax.psum(part.astype(jnp.bfloat16), 'tp')  129 us
    unnamed x288, local copies, waits for them, and re-layouts  49.5 us
    dot_general x16, matrix products, layer_chunk(): jnp.einsum('bst,tbhe->bshe', onehot, new, preferred_element_type=jnp.floa...  34.5 us
    dot_general x8, matrix products, layer_chunk(): jnp.einsum('bhts,bshe->tbhe', probs, v_all, preferred_element_type=jnp.fl...  27.6 us
    slice x16, local copies, waits for them, and re-layouts, apply_rotary(): pairs = vectors[..., :ROT_DIM].reshape(lead_shape + (ROT_DIM // 2, 2))  26 us
    concatenate x16, other arithmetic, apply_rotary(): jnp.concatenate([rotated.reshape(lead_shape + (ROT_DIM,)), vectors[..., R...  17.8 us
    another operation x8, other arithmetic  17 us
  transfers between devices with their start and end apart: 2, of which 2 were waited for; matrix products, arithmetic and copies ran while one was open for 9% of the time, Pallas kernels for 0%

profile of v1, /device:TPU:113, one launch (start us, length us, event | category | flops | bytes accessed | tf_op | source)
XLA Modules:
  0.0 657.8 jit_solution(17575279869579266538)
XLA Ops:
  12.1 4.2 convert_reduce_fusion.7
  18.0 2.7 fusion.52
  22.4 3.7 fusion.194
  26.1 11.1 %fusion.88 = f32[32,16,2048]{2,1,0:T(8,128)} fusion(bf16[2,1024,2048]{2,1,0:T(8,128)(2,1)} %param.26, bf16[2,2048,1024]{2,1,0:T(8,128)(2,1)} %param.24, f32[1024]{0:T(1024)S(1)} %bitcast.582, f32[32,16]{1,0:T(8,128)S(1)} %add_rsqrt_fusion.1, f32[32,16]{1,0:T(8,128)S(1)} %get-tuple-element.143, f32[2048]{0:T(1024)S(1)} %bitcast.547, ...), kind=kOutput, calls=%fused_computation.119 | convolution fusion | flops 4306501632 | bytes 14704640 | tf_op jit(solution)/shard_map/tbd,df->tbf/dot_general | solution.py:41
  37.2 11.1 %fusion.90 = f32[32,16,2048]{2,1,0:T(8,128)} fusion(bf16[2,1024,2048]{2,1,0:T(8,128)(2,1)} %param.26, bf16[2,2048,1024]{2,1,0:T(8,128)(2,1)} %param.24, f32[1024]{0:T(1024)S(1)} %bitcast.583, f32[32,16]{1,0:T(8,128)S(1)} %add_rsqrt_fusion.3, f32[32,16]{1,0:T(8,128)S(1)} %get-tuple-element.144, f32[2048]{0:T(1024)S(1)} %bitcast.548, ...), kind=kOutput, calls=%fused_computation.121 | convolution fusion | flops 4306501632 | bytes 14704640 | tf_op jit(solution)/shard_map/tbd,df->tbf/dot_general | solution.py:41
  48.3 3.5 fusion.206
  54.8 2.9 fusion.190
  57.7 3.7 fusion.202
  64.0 2.9 fusion.192
  66.9 3.5 fusion.204
  70.4 11.1 %fusion.92 = f32[32,16,2048]{2,1,0:T(8,128)} fusion(bf16[2,1024,2048]{2,1,0:T(8,128)(2,1)} %param.26, bf16[2,2048,1024]{2,1,0:T(8,128)(2,1)} %param.24, f32[1024]{0:T(1024)S(1)} %bitcast.584, f32[32,16]{1,0:T(8,128)S(1)} %add_rsqrt_fusion.5, f32[32,16]{1,0:T(8,128)S(1)} %get-tuple-element.145, f32[2048]{0:T(1024)S(1)} %bitcast.554, ...), kind=kOutput, calls=%fused_computation.123 | convolution fusion | flops 4306501632 | bytes 14704640 | tf_op jit(solution)/shard_map/tbd,df->tbf/dot_general | solution.py:41
  81.6 3.4 fusion.218
  85.0 3.5 fusion.214
  88.5 3.4 fusion.216
  93.6 11.2 %fusion.94 = f32[32,16,2048]{2,1,0:T(8,128)} fusion(bf16[2,1024,2048]{2,1,0:T(8,128)(2,1)} %param.26, bf16[2,2048,1024]{2,1,0:T(8,128)(2,1)} %param.24, f32[1024]{0:T(1024)S(1)} %bitcast.585, f32[2048]{0:T(1024)S(1)} %bitcast.558, f32[2048]{0:T(1024)S(1)} %bitcast.574, f32[32,16]{1,0:T(8,128)S(1)} %add_rsqrt_fusion.7, ...), kind=kOutput, calls=%fused_computation.125 | convolution fusion | flops 4306501632 | bytes 14704640 | tf_op jit(solution)/shard_map/tbd,df->tbf/dot_general | solution.py:41
  104.8 3.4 fusion.230
  108.2 3.6 fusion.226
  111.8 3.5 fusion.228
  115.4 9.4 %fusion.485 = (bf16[1,16,128,2,128]{4,3,2,1,0:T(2,128)(2,1)}, bf16[1,16,128,2,128]{4,3,2,1,0:T(2,128)(2,1)}, bf16[1,16,128,2,128]{4,3,2,1,0:T(2,128)(2,1)}, bf16...) fusion(bf16[2,64,128,2,128]{4,3,2,1,0:T(2,128)(2,1)S(1)} %bitca, ...), kind=kLoop, calls=%fused_computation.640 | loop fusion | bytes 16777216 | tf_op jit(solution)/shard_map/slice | solution.py:78
  124.7 9.3 %fusion.484 = (bf16[1,16,128,2,128]{4,3,2,1,0:T(2,128)(2,1)}, bf16[1,16,128,2,128]{4,3,2,1,0:T(2,128)(2,1)}, bf16[1,16,128,2,128]{4,3,2,1,0:T(2,128)(2,1)}, bf16...) fusion(bf16[2,64,128,2,128]{4,3,2,1,0:T(2,128)(2,1)S(1)} %bitca, ...), kind=kLoop, calls=%fused_computation.639 | loop fusion | bytes 16777216 | tf_op jit(solution)/shard_map/slice | solution.py:78
  138.1 5.5 multiply_cosine_fusion.3
  153.5 2.8 fusion.260
  156.3 3.0 fusion.294
  175.3 3.2 fusion.256
  178.5 3.0 fusion.292
  197.4 2.8 fusion.252
  200.2 3.0 fusion.290
  220.5 2.8 fusion.248
  223.4 4.1 fusion.288
  231.2 4.5 add_convert_fusion.1
  244.9 2.3 copy.74
  250.1 92.3 %all-reduce.7.cloned.1.call-done = (bf16[32,16,2048]{2,1,0:T(8,128)(2,1)}, bf16[32,16,2048]{2,1,0:T(8,128)(2,1)}, bf16[32,16,2048]{2,1,0:T(8,128)(2,1)}, bf16[32,16,2048]{2,1,0:T(8,128)(2,1)}) async-done(((bf16[32,16,2048]{2,1,0:T(8,128)(2,1)}, bf16[32,16,2048]{2,1,0:T(8,128)(2,1)}, bf16[32,16,2048]{2,1,0:T(8,128)(2,1)}, bf16[32,16,2048]{2,1,0:T(8,128)(2,1)}), (bf16[32,16,2048]{2,1,0:T(8,128)(2,1)}, ...) | async-done | bytes 8388624 | tf_op jit(solution)/shard_map/psum | solution.py:80
  342.4 9.9 %convert_reduce_fusion.6 = (f32[32,16]{1,0:T(8,128)}, bf16[32,16,2048]{2,1,0:T(8,128)(2,1)}, f32[32,16]{1,0:T(8,128)}, bf16[32,16,2048]{2,1,0:T(8,128)(2,1)}, f3...) fusion(f32[2048]{0:T(1024)S(1)} %bitcast.513, ...), kind=kLoop, calls=%fused_computation.31 | loop fusion | flops 29358080 | bytes 25182208 | tf_op jit(solution)/shard_map/reduce_sum | solution.py:13
  355.0 11.2 %fusion.72 = f32[32,16,2048]{2,1,0:T(8,128)} fusion(bf16[2,1024,2048]{2,1,0:T(8,128)(2,1)} %param.26, bf16[2,2048,1024]{2,1,0:T(8,128)(2,1)} %param.24, f32[1024]{0:T(1024)} %bitcast.578, bf16[32,16,2048]{2,1,0:T(8,128)(2,1)} %copy-done.9, f32[32,16]{1,0:T(8,128)} %add_rsqrt_fusion, f32[32,16]{1,0:T(8,128)} %copy-done.98, f32[2048]{0:T(1024)} %bitcast.514, ...), kind=kOutput, calls=%fused_computation.103 | convolution fusion | flops 4306501632 | bytes 14733312 | tf_op jit(solution)/shard_map/tbd,df->tbf/dot_general | solution.py:41
  366.2 3.6 fusion.188
  371.1 11.1 %fusion.74 = f32[32,16,2048]{2,1,0:T(8,128)} fusion(bf16[2,1024,2048]{2,1,0:T(8,128)(2,1)} %param.26, bf16[2,2048,1024]{2,1,0:T(8,128)(2,1)} %param.24, f32[1024]{0:T(1024)} %bitcast.579, bf16[32,16,2048]{2,1,0:T(8,128)(2,1)} %get-tuple-element.36, f32[32,16]{1,0:T(8,128)} %add_rsqrt_fusion.2, f32[32,16]{1,0:T(8,128)} %copy-done.102, f32[2048]{0:T(1024)} %bitcast.516, ...), kind=kOutput, calls=%fused_computation.105 | convolution fusion | flops 4306501632 | bytes 14733312 | tf_op jit(solution)/shard_map/tbd,df->tbf/dot_general | solution.py:41
  382.3 3.5 fusion.200
  393.8 11.2 %fusion.76 = f32[32,16,2048]{2,1,0:T(8,128)} fusion(bf16[2,1024,2048]{2,1,0:T(8,128)(2,1)} %param.26, bf16[2,2048,1024]{2,1,0:T(8,128)(2,1)} %param.24, f32[1024]{0:T(1024)} %bitcast.580, bf16[32,16,2048]{2,1,0:T(8,128)(2,1)} %get-tuple-element.34, f32[32,16]{1,0:T(8,128)} %add_rsqrt_fusion.4, f32[32,16]{1,0:T(8,128)} %copy-done.104, f32[2048]{0:T(1024)} %bitcast.518, ...), kind=kOutput, calls=%fused_computation.107 | convolution fusion | flops 4306501632 | bytes 14733312 | tf_op jit(solution)/shard_map/tbd,df->tbf/dot_general | solution.py:41
  405.0 3.8 fusion.212
  413.8 11.3 %fusion.78 = f32[32,16,2048]{2,1,0:T(8,128)} fusion(bf16[2,1024,2048]{2,1,0:T(8,128)(2,1)} %param.26, bf16[2,2048,1024]{2,1,0:T(8,128)(2,1)} %param.24, f32[1024]{0:T(1024)} %bitcast.581, bf16[32,16,2048]{2,1,0:T(8,128)(2,1)} %get-tuple-element.26, f32[2048]{0:T(1024)} %bitcast.520, f32[2048]{0:T(1024)} %bitcast.536, f32[32,16]{1,0:T(8,128)} %add_rsqrt_fusion.6, ...), kind=kOutput, calls=%fused_computation.109 | convolution fusion | flops 4306501632 | bytes 14733312 | tf_op jit(solution)/shard_map/tbd,df->tbf/dot_general | solution.py:41
  425.2 3.8 fusion.224
  436.0 2.5 copy.129
  438.5 2.5 subtract_convert_fusion.1
  451.8 3.8 fusion.295
  462.0 2.5 copy.111
  464.6 2.4 subtract_convert_fusion.5
  477.1 3.8 fusion.293
  487.3 2.5 copy.93
  489.8 2.5 subtract_convert_fusion.9
  496.1 2.5 fusion.255
  502.8 3.8 fusion.291
  513.0 2.5 copy.75
  515.6 2.4 subtract_convert_fusion.13
  527.7 3.0 fusion.289
  531.1 4.4 add_convert_fusion
  545.4 3.6 maximum_bitcast_fusion
  553.6 7.6 %pad_maximum_fusion.1 = bf16[2,64,128,2,128]{4,2,3,1,0:T(8,128)(2,1)} fusion(bf16[1,64,128,2,128]{4,2,3,1,0:T(8,128)(2,1)} %maximum_bitcast_fusion.1, bf16[1,64,128,2,128]{4,2,3,1,0:T(8,128)(2,1)} %maximum_bitcast_fusion), kind=kLoop, calls=%fused_computation.9 | loop fusion | flops 4194304 | bytes 16777216 | tf_op jit(solution)/shard_map/stack | solution.py:87
  561.2 16.5 %copy.135 = bf16[2,64,128,2,128]{4,3,2,1,0:T(2,128)(2,1)} copy(bf16[2,64,128,2,128]{4,2,3,1,0:T(8,128)(2,1)} %pad_maximum_fusion.1) | data formatting | bytes 16777216
  577.7 2.3 maximum_bitcast_fusion.3
  580.0 6.3 pad_maximum_fusion.2
  586.4 16.5 %copy.136 = bf16[2,64,128,2,128]{4,3,2,1,0:T(2,128)(2,1)} copy(bf16[2,64,128,2,128]{4,2,3,1,0:T(8,128)(2,1)} %pad_maximum_fusion.2) | data formatting | bytes 16777216
  602.8 36.7 %all-reduce.5.cloned.1.call-done = (bf16[32,16,2048]{2,1,0:T(8,128)(2,1)}, bf16[32,16,2048]{2,1,0:T(8,128)(2,1)}, bf16[32,16,2048]{2,1,0:T(8,128)(2,1)}, bf16[32,16,2048]{2,1,0:T(8,128)(2,1)}) async-done(((bf16[32,16,2048]{2,1,0:T(8,128)(2,1)}, bf16[32,16,2048]{2,1,0:T(8,128)(2,1)}, bf16[32,16,2048]{2,1,0:T(8,128)(2,1)}, bf16[32,16,2048]{2,1,0:T(8,128)(2,1)}), (bf16[32,16,2048]{2,1,0:T(8,128)(2,1)}, ...) | async-done | bytes 8388624 | tf_op jit(solution)/shard_map/psum | solution.py:80
  639.5 7.6 %fusion.59 = (bf16[32,16,2048]{2,1,0:T(8,128)(2,1)S(1)}, bf16[32,16,2048]{2,1,0:T(8,128)(2,1)S(1)}, bf16[32,16,2048]{2,1,0:T(8,128)(2,1)S(1)}, bf16[32,16,2048]{2,1,0:T(8,128)(2,1)S(1)}) fusion(bf16[32,16,2048]{2,1,0:T(8,128)(2,1)S(1)} %copy-done.4, bf16[32,16,2048]{2,1,0:T(8,128)(2,1)} %get-tuple-element.20, f32[2048]{0:T(1024)S(1)} %bitcast.512, ...), kind=kLoop, calls=%fused_computation.86 | loop fusion | flops 20971520 | bytes 25174016 | tf_op jit(solution)/shard_map/convert_element_type | solution.py:82
  647.1 3.6 pad_maximum_fusion
  (468 shorter events, 190.0 us)
Async XLA Ops:
  7.2 335.2 %all-reduce.7.cloned.1.call-start = ((), (), s32[]{:S(2)}) async-start(), calls=%async_computation.1 | async-start | bytes 16777216 | tf_op jit(solution)/shard_map/psum | solution.py:80
  12.1 5.9 copy-start
  22.4 25.9 %copy-start.66 = (bf16[2,128,2048,1]{1,0,2,3:T(2,128)(2,1)}, bf16[2,128,2048,1]{1,0,2,3:T(2,128)(2,1)S(1)}, u32[]{:S(2)}) copy-start(bf16[2,128,2048,1]{1,0,2,3:T(2,128)(2,1)S(1)} %reshape.474) | copy-start | bytes 3145732
  57.7 76.3 %copy-start.47 = (f32[32,16,2,128]{3,1,2,0:T(8,128)}, f32[32,16,2,128]{3,1,2,0:T(8,128)S(1)}, u32[]{:S(2)}) copy-start(f32[32,16,2,128]{3,1,2,0:T(8,128)S(1)} %fusion.190) | copy-start | bytes 1572868
  70.4 11.2 %copy-start.67 = (bf16[2,128,2048,1]{1,0,2,3:T(2,128)(2,1)S(1)}, bf16[2,128,2048,1]{1,0,2,3:T(2,128)(2,1)}, u32[]{:S(2)}) copy-start(bf16[2,128,2048,1]{1,0,2,3:T(2,128)(2,1)} %copy-done.66) | copy-start | bytes 3145732
  108.2 7.1 %slice-start = ((s8[8388608]{0:T(1024)(128)(4,1)}), s8[4194304]{0:T(1024)(128)(4,1)S(1)}, s32[]{:S(2)}) async-start(s8[8388608]{0:T(1024)(128)(4,1)} %bitcast.444), calls=%async_computation.2 | async-start | bytes 8388608
  111.8 12.9 %slice-start.2 = ((s8[8388608]{0:T(1024)(128)(4,1)}), s8[4194304]{0:T(1024)(128)(4,1)S(1)}, s32[]{:S(2)}) async-start(s8[8388608]{0:T(1024)(128)(4,1)} %bitcast.446), calls=%async_computation.4 | async-start | bytes 8388608
  115.3 9.4 %slice-start.3 = ((s8[8388608]{0:T(1024)(128)(4,1)}), s8[4194304]{0:T(1024)(128)(4,1)S(1)}, s32[]{:S(2)}) async-start(s8[8388608]{0:T(1024)(128)(4,1)} %bitcast.446), calls=%async_computation.5 | async-start | bytes 8388608
  144.7 4.9 copy-start.57
  147.3 5.2 copy-start.90
  147.3 6.2 copy-start.96
  147.3 6.2 copy-start.129
  147.3 6.2 copy-start.137
  152.4 8.0 %copy-start.44 = (f32[32,16,2,128]{3,1,2,0:T(8,128)S(1)}, f32[32,16,2,128]{3,1,2,0:T(8,128)}, u32[]{:S(2)}) copy-start(f32[32,16,2,128]{3,1,2,0:T(8,128)} %fusion.202) | copy-start | bytes 1572868
  153.1 8.3 %copy-start.45 = (f32[32,16,2,128]{3,1,2,0:T(8,128)S(1)}, f32[32,16,2,128]{3,1,2,0:T(8,128)}, u32[]{:S(2)}) copy-start(f32[32,16,2,128]{3,1,2,0:T(8,128)} %fusion.204) | copy-start | bytes 1572868
  166.6 4.9 copy-start.56
  169.2 6.0 copy-start.93
  169.2 6.0 copy-start.125
  169.3 6.0 copy-start.135
  174.2 8.4 %copy-start.41 = (f32[32,16,2,128]{3,1,2,0:T(8,128)S(1)}, f32[32,16,2,128]{3,1,2,0:T(8,128)}, u32[]{:S(2)}) copy-start(f32[32,16,2,128]{3,1,2,0:T(8,128)} %fusion.214) | copy-start | bytes 1572868
  174.9 8.7 %copy-start.42 = (f32[32,16,2,128]{3,1,2,0:T(8,128)S(1)}, f32[32,16,2,128]{3,1,2,0:T(8,128)}, u32[]{:S(2)}) copy-start(f32[32,16,2,128]{3,1,2,0:T(8,128)} %fusion.216) | copy-start | bytes 1572868
  188.8 4.9 copy-start.55
  191.4 4.9 copy-start.88
  191.4 6.0 copy-start.127
  191.4 6.0 copy-start.133
  196.3 8.1 %copy-start.38 = (f32[32,16,2,128]{3,1,2,0:T(8,128)S(1)}, f32[32,16,2,128]{3,1,2,0:T(8,128)}, u32[]{:S(2)}) copy-start(f32[32,16,2,128]{3,1,2,0:T(8,128)} %fusion.226) | copy-start | bytes 1572868
  197.0 8.2 %copy-start.39 = (f32[32,16,2,128]{3,1,2,0:T(8,128)S(1)}, f32[32,16,2,128]{3,1,2,0:T(8,128)}, u32[]{:S(2)}) copy-start(f32[32,16,2,128]{3,1,2,0:T(8,128)} %fusion.228) | copy-start | bytes 1572868
  210.4 4.9 copy-start.54
  213.0 7.5 %copy-start.123 = (pred[16,128]{1,0:T(8,128)(4,1)S(1)}, pred[16,128]{1,0:T(8,128)(4,1)}, u32[]{:S(2)}) copy-start(pred[16,128]{1,0:T(8,128)(4,1)} %get-tuple-element.154) | copy-start | bytes 6148
  213.0 7.5 %copy-start.131 = (bf16[32,16,2,128]{3,1,2,0:T(8,128)(2,1)S(1)}, bf16[32,16,2,128]{3,1,2,0:T(8,128)(2,1)}, u32[]{:S(2)}) copy-start(bf16[32,16,2,128]{3,1,2,0:T(8,128)(2,1)} %fusion.230) | copy-start | bytes 786436
  218.1 13.1 %copy-start.1 = (bf16[2,256,2048]{2,1,0:T(8,128)(2,1)S(1)}, bf16[2,256,2048]{2,1,0:T(8,128)(2,1)}, u32[]{:S(2)}) copy-start(bf16[2,256,2048]{2,1,0:T(8,128)(2,1)} %param.23) | copy-start | bytes 6291460
  243.7 395.8 %all-reduce.5.cloned.1.call-start = ((), (), s32[]{:S(2)}) async-start(), calls=%async_computation | async-start | bytes 16777216 | tf_op jit(solution)/shard_map/psum | solution.py:80
  244.9 4.6 copy-start.112
  355.0 11.2 %copy-start.59 = (bf16[2,128,2048,1]{1,0,2,3:T(2,128)(2,1)S(1)}, bf16[2,128,2048,1]{1,0,2,3:T(2,128)(2,1)}, u32[]{:S(2)}) copy-start(bf16[2,128,2048,1]{1,0,2,3:T(2,128)(2,1)} %reshape.482) | copy-start | bytes 3145732
  387.4 45.2 %copy-start.48 = (f32[32,16,2,128]{3,1,2,0:T(8,128)}, f32[32,16,2,128]{3,1,2,0:T(8,128)S(1)}, u32[]{:S(2)}) copy-start(f32[32,16,2,128]{3,1,2,0:T(8,128)S(1)} %fusion.184) | copy-start | bytes 1572868
  390.6 42.8 %copy-start.49 = (f32[32,16,2,128]{3,1,2,0:T(8,128)}, f32[32,16,2,128]{3,1,2,0:T(8,128)S(1)}, u32[]{:S(2)}) copy-start(f32[32,16,2,128]{3,1,2,0:T(8,128)S(1)} %fusion.186) | copy-start | bytes 1572868
  443.6 4.6 copy-start.91
  443.6 6.3 copy-start.53
  443.6 6.3 copy-start.97
  443.6 6.3 copy-start.130
  443.6 6.2 copy-start.138
  448.2 9.4 %copy-start.46 = (f32[32,16,2,128]{3,1,2,0:T(8,128)S(1)}, f32[32,16,2,128]{3,1,2,0:T(8,128)}, u32[]{:S(2)}) copy-start(f32[32,16,2,128]{3,1,2,0:T(8,128)} %fusion.196) | copy-start | bytes 1572868
  469.6 5.7 copy-start.52
  469.6 5.7 copy-start.94
  469.6 5.7 copy-start.126
  469.7 5.7 copy-start.136
  474.2 8.7 %copy-start.43 = (f32[32,16,2,128]{3,1,2,0:T(8,128)S(1)}, f32[32,16,2,128]{3,1,2,0:T(8,128)}, u32[]{:S(2)}) copy-start(f32[32,16,2,128]{3,1,2,0:T(8,128)} %fusion.208) | copy-start | bytes 1572868
  492.3 7.6 %copy-start.89 = (pred[16,32,128]{2,1,0:T(8,128)(4,1)S(1)}, pred[16,32,128]{2,1,0:T(8,128)(4,1)}, u32[]{:S(2)}) copy-start(pred[16,32,128]{2,1,0:T(8,128)(4,1)} %get-tuple-element.151) | copy-start | bytes 196612
  494.9 6.1 copy-start.51
  494.9 6.1 copy-start.128
  494.9 6.1 copy-start.134
  499.9 8.7 %copy-start.40 = (f32[32,16,2,128]{3,1,2,0:T(8,128)S(1)}, f32[32,16,2,128]{3,1,2,0:T(8,128)}, u32[]{:S(2)}) copy-start(f32[32,16,2,128]{3,1,2,0:T(8,128)} %fusion.220) | copy-start | bytes 1572868
  515.6 6.2 copy-start.124
  517.9 5.9 copy-start.58
  520.5 5.3 copy-start.50
  520.5 5.3 copy-start.132
  524.8 6.3 copy-start.82
  530.7 4.8 copy-start.83
  561.2 16.5 %copy-start.78 = (bf16[16,128,2,128]{3,1,2,0:T(8,128)(2,1)S(1)}, bf16[16,128,2,128]{3,1,2,0:T(8,128)(2,1)}, u32[]{:S(2)}) copy-start(bf16[16,128,2,128]{3,1,2,0:T(8,128)(2,1)} %fusion.262) | copy-start | bytes 3145732
  561.2 16.5 %copy-start.79 = (bf16[16,128,2,128]{3,1,2,0:T(8,128)(2,1)S(1)}, bf16[16,128,2,128]{3,1,2,0:T(8,128)(2,1)}, u32[]{:S(2)}) copy-start(bf16[16,128,2,128]{3,1,2,0:T(8,128)(2,1)} %fusion.258) | copy-start | bytes 3145732
  561.2 16.5 %copy-start.80 = (bf16[16,128,2,128]{3,1,2,0:T(8,128)(2,1)S(1)}, bf16[16,128,2,128]{3,1,2,0:T(8,128)(2,1)}, u32[]{:S(2)}) copy-start(bf16[16,128,2,128]{3,1,2,0:T(8,128)(2,1)} %fusion.254) | copy-start | bytes 3145732
  561.2 16.5 %copy-start.81 = (bf16[16,128,2,128]{3,1,2,0:T(8,128)(2,1)S(1)}, bf16[16,128,2,128]{3,1,2,0:T(8,128)(2,1)}, u32[]{:S(2)}) copy-start(bf16[16,128,2,128]{3,1,2,0:T(8,128)(2,1)} %fusion.250) | copy-start | bytes 3145732
  586.4 53.1 %copy-start.4 = (bf16[32,16,2048]{2,1,0:T(8,128)(2,1)S(1)}, bf16[32,16,2048]{2,1,0:T(8,128)(2,1)}, u32[]{:S(2)}) copy-start(bf16[32,16,2048]{2,1,0:T(8,128)(2,1)} %get-tuple-element.26) | copy-start | bytes 6291460
  586.4 53.1 %copy-start.109 = (f32[1,2048]{1,0:T(1,128)S(1)}, f32[1,2048]{1,0:T(1,128)}, u32[]{:S(2)}) copy-start(f32[1,2048]{1,0:T(1,128)} %get-tuple-element.129) | copy-start | bytes 24580
  (81 other events, 214.5 us)
Sparse Core Ops, SparseCore 0:
  243.8 98.4 all-reduce.6
  543.8 95.6 all-reduce.4

commit v2 on v0

v2 whole, which is shorter than its diff:
```python
import functools

import jax
import jax.numpy as jnp
import numpy as np
from jax import lax
from jax.experimental import pallas as pl
from jax.experimental.pallas import tpu as pltpu
from jax.sharding import PartitionSpec as P

ROT_DIM = 64
LN_EPS = 1e-5
SEQS = 8
BLOCK = 16
MESH = pl.DeviceIdType.MESH
F32 = jnp.float32
BF16 = jnp.bfloat16


def rotary_table(n_pos, head_dim):
    inv_freq = 1.0 / (10000.0 ** (jnp.arange(0, ROT_DIM, 2).astype(F32) / ROT_DIM))
    angles = jnp.arange(n_pos).astype(F32)[:, None] * inv_freq[None, :]
    cos, sin = jnp.cos(angles), jnp.sin(angles)
    rest = head_dim - ROT_DIM
    cos = jnp.concatenate([jnp.repeat(cos, 2, axis=1), jnp.ones((n_pos, rest), F32)], axis=1)
    sin = jnp.stack([-sin, sin], axis=-1).reshape(n_pos, ROT_DIM)
    sin = jnp.concatenate([sin, jnp.zeros((n_pos, rest), F32)], axis=1)
    terms = []
    for table in (cos, sin):
        for _ in range(3):
            term = lax.reduce_precision(table, 8, 7)
            terms.append(term.astype(BF16))
            table = table - term
    return jnp.concatenate(terms, axis=1)


def normalise(hid, gain, bias):
    row_mean = jnp.mean(hid, axis=-1, keepdims=True)
    centered = hid - row_mean
    row_var = jnp.mean(centered * centered, axis=-1, keepdims=True)
    return centered * lax.rsqrt(row_var + LN_EPS) * gain + bias


def kernel(dims, cl_s, clv, tab, gain, bias, bout, bin_, x_hbm, k_hbm, v_hbm, wq, wk, wv, win, wo, wout,
           hid_out, k_out, v_out,
           w1, w2, hbuf, own, xown, xbuf, kbuf, vbuf, qkv, cs, ctx, mid, part, arecv, pair, b1r, b2r,
           w_sem, x_sem, xo_sem, kv_sem, kvo_sem, out_sem,
           a_send, a_recv, b1_send, b1_recv, b2_send, b2_recv, g1_send, g1_recv, g2_send, g2_recv, d_send, d_recv):
    n_layers, n_chunks, steps, heads, head_dim, d_model, d_ff = dims
    rows = steps * SEQS
    half = rows // 2
    own_rows = rows // 8
    sub = own_rows // 2
    width = heads * head_dim
    slots2 = k_hbm.shape[2]
    total = n_layers * n_chunks
    me = lax.axis_index("tp")
    core = lax.rem(me, 2)
    chip = lax.div(me, 2)
    left, right = lax.rem(me + 6, 8), lax.rem(me + 2, 8)
    mate = me + 1 - 2 * core
    chip_l, chip_r, chip_o = lax.rem(chip + 3, 4), lax.rem(chip + 1, 4), lax.rem(chip + 2, 4)
    mult = pl.multiple_of

    def block_of(q):
        return mult(q * own_rows, own_rows)

    def rows_of(q):
        return mult(core * half + q * own_rows, own_rows)

    def remote(src, dst, send, recv, dev):
        return pltpu.make_async_remote_copy(src_ref=src, dst_ref=dst, send_sem=send, recv_sem=recv,
                                            device_id={"tp": dev}, device_id_type=MESH)

    barrier = pltpu.get_barrier_semaphore()
    for dev in (left, right, mate):
        pl.semaphore_signal(barrier, inc=1, device_id={"tp": dev}, device_id_type=MESH)

    def weight_copies(layer):
        return [pltpu.make_async_copy(wq.at[layer], w1.at[layer, :, pl.ds(0, width)], w_sem.at[layer, 0]),
                pltpu.make_async_copy(wk.at[layer], w1.at[layer, :, pl.ds(width, width)], w_sem.at[layer, 1]),
                pltpu.make_async_copy(wv.at[layer], w1.at[layer, :, pl.ds(2 * width, width)], w_sem.at[layer, 2]),
                pltpu.make_async_copy(win.at[layer], w1.at[layer, :, pl.ds(3 * width, d_ff)], w_sem.at[layer, 3]),
                pltpu.make_async_copy(wo.at[layer], w2.at[layer, pl.ds(0, width), :], w_sem.at[layer, 4]),
                pltpu.make_async_copy(wout.at[layer], w2.at[layer, pl.ds(width, d_ff), :], w_sem.at[layer, 5])]

    def x_copy(c):
        return pltpu.make_async_copy(x_hbm.at[:, pl.ds(mult(c * SEQS, SEQS), SEQS), :], xbuf.at[lax.rem(c, 2)],
                                     x_sem.at[lax.rem(c, 2)])

    def kv_in(i):
        layer, c, s = lax.div(i, n_chunks), lax.rem(i, n_chunks), lax.rem(i, 2)
        seqs = pl.ds(mult(c * SEQS, SEQS), SEQS)
        return [pltpu.make_async_copy(k_hbm.at[layer, seqs], kbuf.at[s], kv_sem.at[0, s]),
                pltpu.make_async_copy(v_hbm.at[layer, seqs], vbuf.at[s], kv_sem.at[1, s])]

    def kv_back(i):
        layer, c, s = lax.div(i, n_chunks), lax.rem(i, n_chunks), lax.rem(i, 2)
        seqs = pl.ds(mult(c * SEQS, SEQS), SEQS)
        return [pltpu.make_async_copy(kbuf.at[s], k_out.at[layer, seqs], kvo_sem.at[0, s]),
                pltpu.make_async_copy(vbuf.at[s], v_out.at[layer, seqs], kvo_sem.at[1, s])]

    def hid_copy(c):
        return pltpu.make_async_copy(hbuf.at[c], hid_out.at[c], out_sem.at[c])

    steps_own = own_rows // SEQS
    own_copy = pltpu.make_async_copy(x_hbm.at[pl.ds((core * 4 + chip) * steps_own, steps_own)], xown, xo_sem)
    x_copy(0).start()
    for copy in weight_copies(0)[:3]:
        copy.start()
    for copy in kv_in(0):
        copy.start()
    for copy in weight_copies(0)[3:]:
        copy.start()
    own_copy.start()
    for layer in range(1, n_layers):
        for copy in weight_copies(layer):
            copy.start()
    pl.semaphore_wait(barrier, 3)

    def piece_qkv(i):
        layer, c = lax.div(i, n_chunks), lax.rem(i, n_chunks)

        @pl.when(i >= 1)
        def _():
            for copy in kv_back(i - 1):
                copy.wait()

        @pl.when(i + 1 < total)
        def _():
            for copy in kv_in(i + 1):
                copy.start()

        @pl.when(i + 1 < n_chunks)
        def _():
            x_copy(i + 1).start()

        @pl.when(i < n_chunks)
        def _():
            x_copy(i).wait()
            s = lax.rem(c, 2)
            per = BLOCK // SEQS

            def block(j, carry):
                hid = xbuf[s, pl.ds(j * per, per)].astype(F32).reshape(BLOCK, d_model)
                normed = normalise(hid, gain[0].astype(F32), bias[0].astype(F32))
                hbuf[c, pl.ds(mult(j * BLOCK, BLOCK), BLOCK)] = normed.astype(BF16)
                return carry

            lax.fori_loop(0, rows // BLOCK, block, 0)

        for layer_w in range(n_layers):
            @pl.when(i == layer_w * n_chunks)
            def _(layer_w=layer_w):
                for copy in weight_copies(layer_w)[:3]:
                    copy.wait()

        pos = clv[pl.ds(mult(c * SEQS, SEQS), SEQS)][None] + lax.broadcasted_iota(jnp.int32, (steps, SEQS, 128), 0)
        pos = pos.reshape(rows, 128)
        pick = (pos == lax.broadcasted_iota(jnp.int32, (rows, 128), 1)).astype(F32).astype(BF16)
        tabs = jnp.dot(pick, tab[...], preferred_element_type=F32)
        e = head_dim
        cs[:, 0:e] = (tabs[:, 0:e] + tabs[:, e:2 * e]) + tabs[:, 2 * e:3 * e]
        cs[:, e:2 * e] = (tabs[:, 3 * e:4 * e] + tabs[:, 4 * e:5 * e]) + tabs[:, 5 * e:6 * e]
        even = lax.rem(lax.broadcasted_iota(jnp.int32, (rows, e), 1), 2) == 0
        qk = jnp.dot(hbuf[c], w1[layer, :, pl.ds(0, 2 * width)], preferred_element_type=F32)
        for h in range(2 * heads):
            vec = qk[:, h * e:(h + 1) * e]
            other = jnp.where(even, pltpu.roll(vec, e - 1, 1), pltpu.roll(vec, 1, 1))
            qkv[h] = vec * cs[:, 0:e] + other * cs[:, e:2 * e]
        val = jnp.dot(hbuf[c], w1[layer, :, pl.ds(2 * width, width)], preferred_element_type=F32)
        for h in range(heads):
            qkv[2 * heads + h] = val[:, h * e:(h + 1) * e]

    def piece_attend(i):
        layer, c, s = lax.div(i, n_chunks), lax.rem(i, n_chunks), lax.rem(i, 2)
        for copy in kv_in(i):
            copy.wait()
        e = head_dim
        ht = heads * steps
        scale = head_dim ** -0.5
        r_iota = lax.broadcasted_iota(jnp.int32, (slots2, ht), 0)
        j_iota = lax.broadcasted_iota(jnp.int32, (slots2, ht), 1)
        lag = r_iota - heads * lax.rem(j_iota, steps) - lax.div(j_iota, steps)
        slot_row = lax.div(lax.broadcasted_iota(jnp.int32, (slots2, e), 0), heads)
        rr = lax.broadcasted_iota(jnp.int32, (ht, slots2), 1)
        jj = lax.broadcasted_iota(jnp.int32, (ht, slots2), 0)
        seen = jnp.where(lax.rem(rr, heads) == lax.div(jj, steps), lax.div(rr, heads) - lax.rem(jj, steps), 1 << 20)
        for b in range(SEQS):
            n = cl_s[c * SEQS + b]

            def split(first):
                return jnp.concatenate([qkv[first + h, pl.ds(b, steps, stride=SEQS), :] for h in range(heads)],
                                       axis=0).astype(BF16)

            query, key, value = split(0), split(heads), split(2 * heads)
            place = (lag == heads * n).astype(F32).astype(BF16)
            placed = jnp.dot(place, jnp.concatenate([key, value], axis=1), preferred_element_type=F32).astype(BF16)
            fresh = (slot_row >= n) & (slot_row < n + steps)
            k_all = jnp.where(fresh, placed[:, 0:e], kbuf[s, b])
            v_all = jnp.where(fresh, placed[:, e:2 * e], vbuf[s, b])
            kbuf[s, b] = k_all
            vbuf[s, b] = v_all
            scores = lax.dot_general(query, k_all, (((1,), (1,)), ((), ())), preferred_element_type=F32) * scale
            scores = jnp.where(seen <= n, scores, -jnp.inf)
            exp_scores = jnp.exp(scores - jnp.max(scores, axis=-1, keepdims=True))
            probs = (exp_scores / jnp.sum(exp_scores, axis=-1, keepdims=True)).astype(BF16)
            context = jnp.dot(probs, v_all, preferred_element_type=F32)
            for h in range(heads):
                ctx[h, pl.ds(b, steps, stride=SEQS), :] = context[h * steps:(h + 1) * steps]
        for h in range(heads):
            mid[:, h * e:(h + 1) * e] = ctx[h].astype(BF16)
        for copy in kv_back(i):
            copy.start()

    def piece_ff(i):
        layer, c = lax.div(i, n_chunks), lax.rem(i, n_chunks)
        for layer_w in range(n_layers):
            @pl.when(i == layer_w * n_chunks)
            def _(layer_w=layer_w):
                weight_copies(layer_w)[3].wait()
        tile = 512

        def block(j, carry):
            cols = mult(j * tile, tile)
            pre = jnp.dot(hbuf[c], w1[layer, :, pl.ds(mult(3 * width + cols, 256), tile)], preferred_element_type=F32)
            pre = pre + bin_[layer, :, pl.ds(cols, tile)].astype(F32)
            inner = 0.7978845608028654 * (pre + 0.044715 * (pre * pre * pre))
            mid[:, pl.ds(mult(width + cols, 256), tile)] = (pre * (0.5 * (1.0 + jnp.tanh(inner)))).astype(BF16)
            return carry

        lax.fori_loop(0, d_ff // tile, block, 0)

    def piece_out(i):
        layer, s = lax.div(i, n_chunks), lax.rem(i, 2)
        for layer_w in range(n_layers):
            @pl.when(i == layer_w * n_chunks)
            def _(layer_w=layer_w):
                for copy in weight_copies(layer_w)[4:]:
                    copy.wait()
        tile = 512

        def block(j, carry):
            cols = pl.ds(mult(j * tile, tile), tile)
            part[s, :, cols] = jnp.dot(mid[...], w2[layer, :, cols], preferred_element_type=F32).astype(BF16)
            return carry

        lax.fori_loop(0, d_model // tile, block, 0)
        copy_a(i).start()

    def copy_a(u):
        s2, s4 = lax.rem(u, 2), lax.rem(u, 4)
        return remote(part.at[s2, pl.ds(mult((1 - core) * half, half), half)], arecv.at[s4], a_send.at[s2], a_recv.at[s4], mate)

    def copies_b1(u):
        c, s4 = lax.rem(u, n_chunks), lax.rem(u, 4)
        return [remote(pair.at[s4, pl.ds(block_of(chip_o), sub)], b1r.at[0, c], b1_send.at[0, c], b1_recv.at[0, c], left),
                remote(pair.at[s4, pl.ds(mult(block_of(chip_o) + sub, sub), sub)], b1r.at[1, c], b1_send.at[1, c],
                       b1_recv.at[1, c], right)]

    def copies_b2(u):
        c, s4 = lax.rem(u, n_chunks), lax.rem(u, 4)
        return [remote(pair.at[s4, pl.ds(block_of(chip_l), own_rows)], b2r.at[0, c], b2_send.at[0, c], b2_recv.at[0, c], left),
                remote(pair.at[s4, pl.ds(block_of(chip_r), own_rows)], b2r.at[1, c], b2_send.at[1, c], b2_recv.at[1, c], right)]

    def same_rows(c, start, size, send, recv, dev):
        ref = hbuf.at[c, pl.ds(start, size)]
        return remote(ref, ref, send, recv, dev)

    def copies_g1(u):
        c = lax.rem(u, n_chunks)
        mine = rows_of(chip)
        return [same_rows(c, mine, own_rows, g1_send.at[0, c], g1_recv.at[0, c], left),
                same_rows(c, mine, own_rows, g1_send.at[1, c], g1_recv.at[1, c], right),
                same_rows(c, mine, own_rows, d_send.at[0, c], d_recv.at[0, c], mate)]

    def copies_g2(u):
        c = lax.rem(u, n_chunks)
        from_r, from_l = rows_of(chip_r), rows_of(chip_l)
        return [same_rows(c, mult(from_r + sub, sub), sub, g2_send.at[0, c], g2_recv.at[0, c], left),
                same_rows(c, from_l, sub, g2_send.at[1, c], g2_recv.at[1, c], right),
                same_rows(c, from_r, own_rows, d_send.at[1, c], d_recv.at[1, c], mate),
                same_rows(c, from_l, own_rows, d_send.at[2, c], d_recv.at[2, c], mate)]

    def copy_g3(u):
        c = lax.rem(u, n_chunks)
        return same_rows(c, rows_of(chip_o), own_rows, d_send.at[3, c], d_recv.at[3, c], mate)

    def stage_b1(u):
        s2, s4 = lax.rem(u, 2), lax.rem(u, 4)
        copy_a(u).wait()

        def add(start):
            src = pl.ds(mult(core * half + start, BLOCK), BLOCK)
            dst = pl.ds(mult(start, BLOCK), BLOCK)
            pair[s4, dst] = (part[s2, src].astype(F32) + arecv[s4, dst].astype(F32)).astype(BF16)

        for t in range(own_rows // BLOCK):
            add(block_of(chip_o) + t * BLOCK)
        for copy in copies_b1(u):
            copy.start()
        for q in (chip_l, chip_r, chip):
            for t in range(own_rows // BLOCK):
                add(block_of(q) + t * BLOCK)

    def stage_b2(u):
        c, s4 = lax.rem(u, n_chunks), lax.rem(u, 4)
        first, second = copies_b1(u), copies_b2(u)
        first[0].wait_recv()
        dst = pl.ds(block_of(chip_l), sub)
        pair[s4, dst] = (pair[s4, dst].astype(F32) + b1r[0, c].astype(F32)).astype(BF16)
        second[0].start()
        first[1].wait_recv()
        dst = pl.ds(mult(block_of(chip_r) + sub, sub), sub)
        pair[s4, dst] = (pair[s4, dst].astype(F32) + b1r[1, c].astype(F32)).astype(BF16)
        second[1].start()

    def stage_b3(u):
        layer, c, s4 = lax.div(u, n_chunks), lax.rem(u, n_chunks), lax.rem(u, 4)
        for copy in copies_b2(u):
            copy.wait_recv()
        for t in range(own_rows // BLOCK):
            src = pl.ds(mult(block_of(chip) + t * BLOCK, BLOCK), BLOCK)
            loc = pl.ds(t * BLOCK, BLOCK)
            hid = own[c, loc].astype(F32) + bout[layer].astype(F32)
            hid = hid + (pair[s4, src].astype(F32) + (b2r[0, c, loc].astype(F32) + b2r[1, c, loc].astype(F32)))
            hid = hid.astype(BF16)
            dst = pl.ds(mult(rows_of(chip) + t * BLOCK, BLOCK), BLOCK)

            @pl.when(layer + 1 < n_layers)
            def _():
                own[c, loc] = hid
                nxt = layer + 1
                hbuf[c, dst] = normalise(hid.astype(F32), gain[nxt].astype(F32), bias[nxt].astype(F32)).astype(BF16)

            @pl.when(layer + 1 >= n_layers)
            def _():
                hbuf[c, dst] = hid

        for copy in copies_g1(u):
            copy.start()
        for copy in copies_b1(u) + copies_b2(u):
            copy.wait_send()

    def stage_g2(u):
        first, second = copies_g1(u), copies_g2(u)
        c = lax.rem(u, n_chunks)
        same_rows(c, rows_of(chip_r), own_rows, g1_send.at[0, c], g1_recv.at[0, c], left).wait_recv()
        second[0].start()
        second[2].start()
        same_rows(c, rows_of(chip_l), own_rows, g1_send.at[1, c], g1_recv.at[1, c], right).wait_recv()
        second[1].start()
        second[3].start()

    def stage_g3(u):
        c = lax.rem(u, n_chunks)
        theirs = rows_of(chip_o)
        same_rows(c, mult(theirs + sub, sub), sub, g2_send.at[0, c], g2_recv.at[0, c], left).wait_recv()
        same_rows(c, theirs, sub, g2_send.at[1, c], g2_recv.at[1, c], right).wait_recv()
        copy_g3(u).start()

    def stage_g4(u):
        c = lax.rem(u, n_chunks)
        for n, q in enumerate((chip, chip_r, chip_l, chip_o)):
            start = mult((1 - core) * half + q * own_rows, own_rows)
            same_rows(c, start, own_rows, d_send.at[n, c], d_recv.at[n, c], mate).wait_recv()
        for copy in copies_g1(u) + copies_g2(u) + [copy_g3(u)]:
            copy.wait_send()

        @pl.when(u >= total - n_chunks)
        def _():
            hid_copy(c).start()

    def guarded(stage, u):
        @pl.when((u >= 0) & (u < total))
        def _():
            stage(u)

    own_copy.wait()
    for c in range(n_chunks):
        own[c] = xown[:, c * SEQS:(c + 1) * SEQS].astype(F32).reshape(own_rows, d_model).astype(BF16)

    def tick(i, carry):
        guarded(stage_g2, i - 4)
        guarded(piece_qkv, i)
        guarded(stage_b3, i - 3)
        guarded(stage_g3, i - 5)
        guarded(piece_attend, i)
        guarded(stage_b2, i - 2)
        guarded(stage_g4, i - 6)
        guarded(piece_ff, i)
        guarded(stage_b1, i - 1)
        guarded(piece_out, i)
        return carry

    lax.fori_loop(0, total + 6, tick, 0)
    for copy in kv_back(total - 1):
        copy.wait()
    for c in range(n_chunks):
        hid_copy(c).wait()


def decode_shard(x_steps, cur_len, k_cache, v_cache, ln_gain, ln_bias, w_q, w_k, w_v, w_o, w_in, b_in, w_out, b_out):
    steps, batch, d_model = x_steps.shape
    n_layers, _, slots, heads, head_dim = k_cache.shape
    d_ff = w_in.shape[2]
    n_chunks = batch // SEQS
    rows = steps * SEQS
    width = heads * head_dim
    own_rows = rows // 8
    tab = rotary_table(128, head_dim)
    cl_rows = jnp.broadcast_to(cur_len[:, None], (batch, 128))
    k_rows = k_cache.reshape(n_layers, batch, slots * heads, head_dim)
    v_rows = v_cache.reshape(n_layers, batch, slots * heads, head_dim)
    vmem = pl.BlockSpec(memory_space=pltpu.VMEM)
    hbm = pl.BlockSpec(memory_space=pl.ANY)
    dims = (n_layers, n_chunks, steps, heads, head_dim, d_model, d_ff)
    dma = pltpu.SemaphoreType.DMA
    hid, k_new, v_new = pl.pallas_call(
        functools.partial(kernel, dims),
        out_shape=(jax.ShapeDtypeStruct((n_chunks, rows, d_model), BF16),
                   jax.ShapeDtypeStruct(k_rows.shape, BF16), jax.ShapeDtypeStruct(v_rows.shape, BF16)),
        in_specs=[pl.BlockSpec(memory_space=pltpu.SMEM)] + [vmem] * 6 + [hbm] * 9,
        out_specs=(hbm, hbm, hbm),
        scratch_shapes=[
            pltpu.VMEM((n_layers, d_model, 3 * width + d_ff), BF16),
            pltpu.VMEM((n_layers, width + d_ff, d_model), BF16),
            pltpu.VMEM((n_chunks, rows, d_model), BF16),
            pltpu.VMEM((n_chunks, own_rows, d_model), BF16),
            pltpu.VMEM((own_rows // SEQS, batch, d_model), BF16),
            pltpu.VMEM((2, steps, SEQS, d_model), BF16),
            pltpu.VMEM((2, SEQS, slots * heads, head_dim), BF16),
            pltpu.VMEM((2, SEQS, slots * heads, head_dim), BF16),
            pltpu.VMEM((3 * heads, rows, head_dim), F32),
            pltpu.VMEM((rows, 2 * head_dim), F32),
            pltpu.VMEM((heads, rows, head_dim), F32),
            pltpu.VMEM((rows, width + d_ff), BF16),
            pltpu.VMEM((2, rows, d_model), BF16),
            pltpu.VMEM((4, rows // 2, d_model), BF16),
            pltpu.VMEM((4, rows // 2, d_model), BF16),
            pltpu.VMEM((2, n_chunks, own_rows // 2, d_model), BF16),
            pltpu.VMEM((2, n_chunks, own_rows, d_model), BF16),
            dma((n_layers, 6)), dma((2,)), dma, dma((2, 2)), dma((2, 2)), dma((n_chunks,)),
            dma((2,)), dma((4,)), dma((2, n_chunks)), dma((2, n_chunks)), dma((2, n_chunks)), dma((2, n_chunks)),
            dma((2, n_chunks)), dma((2, n_chunks)), dma((2, n_chunks)), dma((2, n_chunks)),
            dma((4, n_chunks)), dma((4, n_chunks)),
        ],
        compiler_params=pltpu.CompilerParams(collective_id=0, has_side_effects=True, vmem_limit_bytes=67043328),
    )(cur_len, cl_rows, tab, ln_gain[:, None, :], ln_bias[:, None, :], b_out[:, None, :], b_in[:, None, :], x_steps, k_rows, v_rows,
      w_q, w_k, w_v, w_in, w_o, w_out)
    hidden = hid.reshape(n_chunks, steps, SEQS, d_model).transpose(1, 0, 2, 3).reshape(steps, batch, d_model)
    return hidden, k_new.reshape(k_cache.shape), v_new.reshape(v_cache.shape)


def solution(mesh):
    cache_spec = P(None, "dp", None, "tp", None)
    in_specs = (P(None, "dp", None), P("dp"), cache_spec, cache_spec, P(None, None), P(None, None),
                P(None, None, "tp"), P(None, None, "tp"), P(None, None, "tp"), P(None, "tp", None),
                P(None, None, "tp"), P(None, "tp"), P(None, "tp", None), P(None, None))
    out_specs = (P(None, "dp", None), cache_spec, cache_spec)
    return jax.shard_map(decode_shard, mesh=mesh, in_specs=in_specs, out_specs=out_specs, check_vma=False)
```

time: 5990 us -> 260 us (0.04)
  local copies, waits for them, and re-layouts: 2840 us -> 27 us
  waiting for transfers between devices: 1500 us -> 0 us
  matrix products: 1170 us -> 0 us
  other arithmetic: 397 us -> 4.05 us
  Pallas kernels: 0 us -> 228 us
    psum x33 -> x0, waiting for transfers between devices: 1500 us -> none  [decode_shard(): layer_sum = lax.psum(layer_part.astype(jnp.bfloat16), 'tp')]
    squeeze x128 -> x0, local copies, waits for them, and re-layouts: 1320 us -> none  [the longest x64 666 us: layer_update(): v_cache[layer_idx]]
    dot_general x448 -> x0, matrix products: 1170 us -> none  [the longest x64 381 us: layer_update(): jnp.dot(gelu_act, out_weight, preferred_element_type=jnp.float32)]
    scatter x128 -> x0, local copies, waits for them, and re-layouts: 1140 us -> none  [the longest x64 581 us: layer_update(): k_cache = k_cache.at[layer_idx, batch_rows, new_pos].set(key_new)]
    pallas_call x0 -> x1, Pallas kernels: none -> 228 us  [decode_shard(): pl.pallas_call(functools.partial(kernel, dims), out_shape=(jax.ShapeDtype...]
    slice x256 -> x0, local copies, waits for them, and re-layouts: 169 us -> none  [the longest x128 94.5 us: apply_rotary(): pairs = vectors[..., :ROT_DIM].reshape(lead_shape + (ROT_DIM // 2, 2))]
    another operation x193 -> x1, other arithmetic: 127 us -> 0.01 us  [rotary_table(): sin = jnp.stack([-sin, sin], axis=-1).reshape(n_pos, ROT_DIM)]
    reshape x192 -> x3, local copies, waits for them, and re-layouts: 132 us -> 8.78 us  [the longest x1 8.59 us: decode_shard(): hid.reshape(n_chunks, steps, SEQS, d_model).transpose(1, 0, 2, 3)]
  transfers between devices with their start and end apart: 33 -> 0, of which waited for: 32 -> 0; matrix products, arithmetic and copies ran while one was open for 16% -> 0% of each run, Pallas kernels for 0% -> 0%
where the time goes in v2:
time: 260 us; the launch traced here: 259 us
  Pallas kernels  228 us (88%)
  local copies, waits for them, and re-layouts  27 us (10%)
  other arithmetic  4.05 us (2%)
    pallas_call x1, Pallas kernels, decode_shard(): pl.pallas_call(functools.partial(kernel, dims), out_shape=(jax.ShapeDtype...  228 us
    unnamed x6, local copies, waits for them, and re-layouts  11.6 us
    reshape x1, local copies, waits for them, and re-layouts, decode_shard(): hid.reshape(n_chunks, steps, SEQS, d_model).transpose(1, 0, 2, 3)  8.59 us

profile of v2, /device:TPU:113, one launch (start us, length us, event | category | flops | bytes accessed | tf_op | source)
XLA Modules:
  0.0 259.4 jit_solution(14644212148102349790)
XLA Ops:
  0.7 1.3 copy.31.bin_
  1.9 0.1 multiply_cosine_fusion
  2.1 1.3 copy.28.gain
  3.4 1.3 copy.29.bias
  4.7 1.3 copy.30.bout
  6.0 0.1 fusion.10
  6.2 0.1 copy.27
  6.3 0.1 copy.25
  6.4 1.4 broadcast_in_dim.12.clv
  7.8 0.6 fusion.6
  8.4 0.6 fusion.7
  9.0 0.6 fusion.5
  9.7 0.6 fusion.8
  10.3 0.6 fusion.9
  10.9 0.6 fusion.4.tab
  11.5 227.6 %shard_map.157 = (bf16[8,256,2048]{2,1,0:T(8,128)(2,1)}, bf16[2,64,256,128]{3,2,1,0:T(8,128)(2,1)}, bf16[2,64,256,128]{3,2,1,0:T(8,128)(2,1)}) custom-call(s32[64]{0:T(128)} %cl_s.1, s32[64,128]{1,0:T(8,128)} %broadcast_in_dim.12.clv, bf16[128,768]{1,0:T(8,128)(2,1)} %fusion.4.tab, bf16[2,1,2048]{2,1,0:T(2,128)(2,1)} %copy.28.gain, ...), custom_call_target="tpu_custom_call" | custom-call | tf_op jit(solution)/shard_map/pallas_call | solution.py:419
  239.2 0.0 slice-start
  239.2 8.6 %copy_bitcast_fusion = bf16[32,64,2048]{2,1,0:T(8,128)(2,1)} fusion(bf16[8,256,2048]{2,1,0:T(8,128)(2,1)} %get-tuple-element.6), kind=kLoop, calls=%fused_computation | loop fusion | bytes 16777216 | tf_op jit(solution)/shard_map/reshape | solution.py:451
  247.8 0.0 slice-start.1
  247.8 8.2 %copy.41 = bf16[2,64,128,2,128]{4,3,2,1,0:T(2,128)(2,1)} copy(bf16[2,64,128,2,128]{4,3,2,1,0:T(2,128)(2,1)} %bitcast.20) | data formatting | bytes 16777216
  256.0 0.0 slice-done
  256.0 0.0 slice-done.1
  256.0 3.4 %copy.42 = bf16[2,64,128,2,128]{4,3,2,1,0:T(2,128)(2,1)} copy(bf16[2,64,128,2,128]{4,3,2,1,0:T(2,128)(2,1)S(1)} %bitcast.19) | data formatting | bytes 16777216
  (6 shorter events, 0.1 us)
Async XLA Ops:
  239.2 16.8 %slice-start = ((s8[8388608]{0:T(1024)(128)(4,1)}), s8[4194304]{0:T(1024)(128)(4,1)S(1)}, s32[]{:S(2)}) async-start(s8[8388608]{0:T(1024)(128)(4,1)} %bitcast.17), calls=%async_computation | async-start | bytes 8388608
  247.8 8.2 %slice-start.1 = ((s8[8388608]{0:T(1024)(128)(4,1)}), s8[4194304]{0:T(1024)(128)(4,1)S(1)}, s32[]{:S(2)}) async-start(s8[8388608]{0:T(1024)(128)(4,1)} %bitcast.17), calls=%async_computation.1 | async-start | bytes 8388608

commit v3 on v2

--- a/solution.py
+++ b/solution.py
@@ -11,27 +11,29 @@
 ROT_DIM = 64
 LN_EPS = 1e-5
 SEQS = 8
+GROUP = 8
 BLOCK = 16
+SCHEDULE = (("qkv", 0), ("b1", 1), ("g2", 3), ("g4", 4), ("mid", 0), ("b3", 2), ("out", 0), ("b2", 1), ("g3", 3))
 MESH = pl.DeviceIdType.MESH
 F32 = jnp.float32
 BF16 = jnp.bfloat16
 
 
 def rotary_table(n_pos, head_dim):
-    inv_freq = 1.0 / (10000.0 ** (jnp.arange(0, ROT_DIM, 2).astype(F32) / ROT_DIM))
-    angles = jnp.arange(n_pos).astype(F32)[:, None] * inv_freq[None, :]
-    cos, sin = jnp.cos(angles), jnp.sin(angles)
+    inv_freq = (1.0 / np.power(10000.0, np.arange(0, ROT_DIM, 2) / ROT_DIM)).astype(np.float32)
+    angles = (np.arange(n_pos, dtype=np.float32)[:, None] * inv_freq[None, :]).astype(np.float64)
+    cos, sin = np.repeat(np.cos(angles), 2, axis=1), np.repeat(np.sin(angles), 2, axis=1)
+    sin[:, 0::2] *= -1.0
     rest = head_dim - ROT_DIM
-    cos = jnp.concatenate([jnp.repeat(cos, 2, axis=1), jnp.ones((n_pos, rest), F32)], axis=1)
-    sin = jnp.stack([-sin, sin], axis=-1).reshape(n_pos, ROT_DIM)
-    sin = jnp.concatenate([sin, jnp.zeros((n_pos, rest), F32)], axis=1)
+    cos = np.concatenate([cos, np.ones((n_pos, rest))], axis=1).astype(np.float32)
+    sin = np.concatenate([sin, np.zeros((n_pos, rest))], axis=1).astype(np.float32)
     terms = []
     for table in (cos, sin):
         for _ in range(3):
-            term = lax.reduce_precision(table, 8, 7)
-            terms.append(term.astype(BF16))
-            table = table - term
-    return jnp.concatenate(terms, axis=1)
+            term = table.astype(BF16)
+            terms.append(term)
+            table = table - term.astype(np.float32)
+    return np.concatenate(terms, axis=1)
 
 
 def normalise(hid, gain, bias):
@@ -41,11 +43,12 @@
     return centered * lax.rsqrt(row_var + LN_EPS) * gain + bias
 
 
-def kernel(dims, cl_s, clv, tab, gain, bias, bout, bin_, x_hbm, k_hbm, v_hbm, wq, wk, wv, win, wo, wout,
+def kernel(dims, cl_s, tab, gain_in, bias_in, bout_in, bin_in, x_hbm, k_hbm, v_hbm, wq, wk, wv, win, wo, wout,
            hid_out, k_out, v_out,
-           w1, w2, hbuf, own, xown, xbuf, kbuf, vbuf, qkv, cs, ctx, mid, part, arecv, pair, b1r, b2r,
+           gain, bias, bout, bin_, w1, w2, hbuf, own, xown, xbuf, kbuf, vbuf, qkv, cs, ctx, mid, part, arecv, pair, b1r, b2r,
            w_sem, x_sem, xo_sem, kv_sem, kvo_sem, out_sem,
-           a_send, a_recv, b1_send, b1_recv, b2_send, b2_recv, g1_send, g1_recv, g2_send, g2_recv, d_send, d_recv):
+           a_send, a_recv, b1_send, b1_recv, b2_send, b2_recv, g1_send, g1_recv, g2_send, g2_recv, d_send, d_recv,
+           bd_send, bd_recv, gn_send, gn_recv):
     n_layers, n_chunks, steps, heads, head_dim, d_model, d_ff = dims
     rows = steps * SEQS
     half = rows // 2
@@ -113,10 +116,10 @@
     for copy in weight_copies(0)[3:]:
         copy.start()
     own_copy.start()
-    for layer in range(1, n_layers):
-        for copy in weight_copies(layer):
-            copy.start()
-    pl.semaphore_wait(barrier, 3)
+
+    for layer in range(n_layers):
+        for dst, src in ((gain, gain_in), (bias, bias_in), (bout, bout_in), (bin_, bin_in)):
+            dst[layer] = src[layer:layer + 1].astype(F32)
 
     def piece_qkv(i):
         layer, c = lax.div(i, n_chunks), lax.rem(i, n_chunks)
@@ -143,11 +146,11 @@
 
             def block(j, carry):
                 hid = xbuf[s, pl.ds(j * per, per)].astype(F32).reshape(BLOCK, d_model)
-                normed = normalise(hid, gain[0].astype(F32), bias[0].astype(F32))
+                normed = normalise(hid, gain[0], bias[0])
                 hbuf[c, pl.ds(mult(j * BLOCK, BLOCK), BLOCK)] = normed.astype(BF16)
                 return carry
 
-            lax.fori_loop(0, rows // BLOCK, block, 0)
+            lax.fori_loop(0, rows // BLOCK, block, 0, unroll=8)
 
         for layer_w in range(n_layers):
             @pl.when(i == layer_w * n_chunks)
@@ -155,8 +158,10 @@
                 for copy in weight_copies(layer_w)[:3]:
                     copy.wait()
 
-        pos = clv[pl.ds(mult(c * SEQS, SEQS), SEQS)][None] + lax.broadcasted_iota(jnp.int32, (steps, SEQS, 128), 0)
-        pos = pos.reshape(rows, 128)
+        row = lax.broadcasted_iota(jnp.int32, (rows, 128), 0)
+        pos = lax.div(row, SEQS)
+        for b in range(SEQS):
+            pos = pos + jnp.where(lax.rem(row, SEQS) == b, cl_s[c * SEQS + b], 0)
         pick = (pos == lax.broadcasted_iota(jnp.int32, (rows, 128), 1)).astype(F32).astype(BF16)
         tabs = jnp.dot(pick, tab[...], preferred_element_type=F32)
         e = head_dim
@@ -172,6 +177,16 @@
         for h in range(heads):
             qkv[2 * heads + h] = val[:, h * e:(h + 1) * e]
 
+    def piece_mid(i):
+        for layer_w in range(n_layers):
+            @pl.when(i == layer_w * n_chunks)
+            def _(layer_w=layer_w):
+                for copy in weight_copies(layer_w)[3:]:
+                    copy.wait()
+
+        piece_ff(i)
+        piece_attend(i)
+
     def piece_attend(i):
         layer, c, s = lax.div(i, n_chunks), lax.rem(i, n_chunks), lax.rem(i, 2)
         for copy in kv_in(i):
@@ -186,28 +201,32 @@
         rr = lax.broadcasted_iota(jnp.int32, (ht, slots2), 1)
         jj = lax.broadcasted_iota(jnp.int32, (ht, slots2), 0)
         seen = jnp.where(lax.rem(rr, heads) == lax.div(jj, steps), lax.div(rr, heads) - lax.rem(jj, steps), 1 << 20)
-        for b in range(SEQS):
-            n = cl_s[c * SEQS + b]
-
-            def split(first):
-                return jnp.concatenate([qkv[first + h, pl.ds(b, steps, stride=SEQS), :] for h in range(heads)],
-                                       axis=0).astype(BF16)
-
-            query, key, value = split(0), split(heads), split(2 * heads)
-            place = (lag == heads * n).astype(F32).astype(BF16)
-            placed = jnp.dot(place, jnp.concatenate([key, value], axis=1), preferred_element_type=F32).astype(BF16)
-            fresh = (slot_row >= n) & (slot_row < n + steps)
-            k_all = jnp.where(fresh, placed[:, 0:e], kbuf[s, b])
-            v_all = jnp.where(fresh, placed[:, e:2 * e], vbuf[s, b])
-            kbuf[s, b] = k_all
-            vbuf[s, b] = v_all
-            scores = lax.dot_general(query, k_all, (((1,), (1,)), ((), ())), preferred_element_type=F32) * scale
-            scores = jnp.where(seen <= n, scores, -jnp.inf)
-            exp_scores = jnp.exp(scores - jnp.max(scores, axis=-1, keepdims=True))
-            probs = (exp_scores / jnp.sum(exp_scores, axis=-1, keepdims=True)).astype(BF16)
-            context = jnp.dot(probs, v_all, preferred_element_type=F32)
-            for h in range(heads):
-                ctx[h, pl.ds(b, steps, stride=SEQS), :] = context[h * steps:(h + 1) * steps]
+
+        def split(b, first):
+            return jnp.concatenate([qkv[first + h, pl.ds(b, steps, stride=SEQS), :] for h in range(heads)], axis=0).astype(BF16)
+
+        for g in range(0, SEQS, GROUP):
+            group = range(g, g + GROUP)
+            lens = [cl_s[c * SEQS + b] for b in group]
+            placed = [jnp.dot((lag == heads * n).astype(F32).astype(BF16),
+                              jnp.concatenate([split(b, heads), split(b, 2 * heads)], axis=1),
+                              preferred_element_type=F32).astype(BF16) for b, n in zip(group, lens)]
+            queries = [split(b, 0) for b in group]
+            fresh = [(slot_row >= n) & (slot_row < n + steps) for n in lens]
+            k_all = [jnp.where(f, p[:, 0:e], kbuf[s, b]) for b, f, p in zip(group, fresh, placed)]
+            v_all = [jnp.where(f, p[:, e:2 * e], vbuf[s, b]) for b, f, p in zip(group, fresh, placed)]
+            scores = [lax.dot_general(q, k, (((1,), (1,)), ((), ())), preferred_element_type=F32) * scale
+                      for q, k in zip(queries, k_all)]
+            for b, k, v in zip(group, k_all, v_all):
+                kbuf[s, b] = k
+                vbuf[s, b] = v
+            scores = [jnp.where(seen <= n, sc, -jnp.inf) for sc, n in zip(scores, lens)]
+            exps = [jnp.exp(sc - jnp.max(sc, axis=-1, keepdims=True)) for sc in scores]
+            probs = [(ex / jnp.sum(ex, axis=-1, keepdims=True)).astype(BF16) for ex in exps]
+            contexts = [jnp.dot(p, v, preferred_element_type=F32) for p, v in zip(probs, v_all)]
+            for b, context in zip(group, contexts):
+                for h in range(heads):
+                    ctx[h, pl.ds(b, steps, stride=SEQS), :] = context[h * steps:(h + 1) * steps]
         for h in range(heads):
             mid[:, h * e:(h + 1) * e] = ctx[h].astype(BF16)
         for copy in kv_back(i):
@@ -215,29 +234,20 @@
 
     def piece_ff(i):
         layer, c = lax.div(i, n_chunks), lax.rem(i, n_chunks)
-        for layer_w in range(n_layers):
-            @pl.when(i == layer_w * n_chunks)
-            def _(layer_w=layer_w):
-                weight_copies(layer_w)[3].wait()
         tile = 512
 
         def block(j, carry):
             cols = mult(j * tile, tile)
             pre = jnp.dot(hbuf[c], w1[layer, :, pl.ds(mult(3 * width + cols, 256), tile)], preferred_element_type=F32)
-            pre = pre + bin_[layer, :, pl.ds(cols, tile)].astype(F32)
+            pre = pre + bin_[layer, :, pl.ds(cols, tile)]
             inner = 0.7978845608028654 * (pre + 0.044715 * (pre * pre * pre))
             mid[:, pl.ds(mult(width + cols, 256), tile)] = (pre * (0.5 * (1.0 + jnp.tanh(inner)))).astype(BF16)
             return carry
 
-        lax.fori_loop(0, d_ff // tile, block, 0)
+        lax.fori_loop(0, d_ff // tile, block, 0, unroll=True)
 
     def piece_out(i):
         layer, s = lax.div(i, n_chunks), lax.rem(i, 2)
-        for layer_w in range(n_layers):
-            @pl.when(i == layer_w * n_chunks)
-            def _(layer_w=layer_w):
-                for copy in weight_copies(layer_w)[4:]:
-                    copy.wait()
         tile = 512
 
         def block(j, carry):
@@ -245,7 +255,7 @@
             part[s, :, cols] = jnp.dot(mid[...], w2[layer, :, cols], preferred_element_type=F32).astype(BF16)
             return carry
 
-        lax.fori_loop(0, d_model // tile, block, 0)
+        lax.fori_loop(0, d_model // tile, block, 0, unroll=True)
         copy_a(i).start()
 
     def copy_a(u):
@@ -258,10 +268,19 @@
                 remote(pair.at[s4, pl.ds(mult(block_of(chip_o) + sub, sub), sub)], b1r.at[1, c], b1_send.at[1, c],
                        b1_recv.at[1, c], right)]
 
+    def copies_bd(u):
+        c, s4 = lax.rem(u, n_chunks), lax.rem(u, 4)
+        return [remote(pair.at[s4, pl.ds(mult(block_of(chip_l) + sub, sub), sub)], b2r.at[0, c, pl.ds(sub, sub)],
+                       bd_send.at[0, c], bd_recv.at[0, c], left),
+                remote(pair.at[s4, pl.ds(block_of(chip_r), sub)], b2r.at[1, c, pl.ds(0, sub)],
+                       bd_send.at[1, c], bd_recv.at[1, c], right)]
+
     def copies_b2(u):
         c, s4 = lax.rem(u, n_chunks), lax.rem(u, 4)
-        return [remote(pair.at[s4, pl.ds(block_of(chip_l), own_rows)], b2r.at[0, c], b2_send.at[0, c], b2_recv.at[0, c], left),
-                remote(pair.at[s4, pl.ds(block_of(chip_r), own_rows)], b2r.at[1, c], b2_send.at[1, c], b2_recv.at[1, c], right)]
+        return [remote(pair.at[s4, pl.ds(block_of(chip_l), sub)], b2r.at[0, c, pl.ds(0, sub)],
+                       b2_send.at[0, c], b2_recv.at[0, c], left),
+                remote(pair.at[s4, pl.ds(mult(block_of(chip_r) + sub, sub), sub)], b2r.at[1, c, pl.ds(sub, sub)],
+                       b2_send.at[1, c], b2_recv.at[1, c], right)]
 
     def same_rows(c, start, size, send, recv, dev):
         ref = hbuf.at[c, pl.ds(start, size)]
@@ -270,8 +289,11 @@
     def copies_g1(u):
         c = lax.rem(u, n_chunks)
         mine = rows_of(chip)
-        return [same_rows(c, mine, own_rows, g1_send.at[0, c], g1_recv.at[0, c], left),
-                same_rows(c, mine, own_rows, g1_send.at[1, c], g1_recv.at[1, c], right),
+        other = mult(mine + sub, sub)
+        return [same_rows(c, other, sub, g1_send.at[0, c], g1_recv.at[0, c], left),
+                same_rows(c, mine, sub, g1_send.at[1, c], g1_recv.at[1, c], right),
+                same_rows(c, mine, sub, gn_send.at[0, c], gn_recv.at[0, c], left),
+                same_rows(c, other, sub, gn_send.at[1, c], gn_recv.at[1, c], right),
                 same_rows(c, mine, own_rows, d_send.at[0, c], d_recv.at[0, c], mate)]
 
     def copies_g2(u):
@@ -299,9 +321,14 @@
             add(block_of(chip_o) + t * BLOCK)
         for copy in copies_b1(u):
             copy.start()
-        for q in (chip_l, chip_r, chip):
-            for t in range(own_rows // BLOCK):
-                add(block_of(q) + t * BLOCK)
+        add(block_of(chip_l) + sub)
+        add(block_of(chip_r))
+        for copy in copies_bd(u):
+            copy.start()
+        add(block_of(chip_l))
+        add(block_of(chip_r) + sub)
+        for t in range(own_rows // BLOCK):
+            add(block_of(chip) + t * BLOCK)
 
     def stage_b2(u):
         c, s4 = lax.rem(u, n_chunks), lax.rem(u, 4)
@@ -317,12 +344,12 @@
 
     def stage_b3(u):
         layer, c, s4 = lax.div(u, n_chunks), lax.rem(u, n_chunks), lax.rem(u, 4)
-        for copy in copies_b2(u):
+        for copy in copies_bd(u) + copies_b2(u):
             copy.wait_recv()
         for t in range(own_rows // BLOCK):
             src = pl.ds(mult(block_of(chip) + t * BLOCK, BLOCK), BLOCK)
             loc = pl.ds(t * BLOCK, BLOCK)
-            hid = own[c, loc].astype(F32) + bout[layer].astype(F32)
+            hid = own[c, loc].astype(F32) + bout[layer]
             hid = hid + (pair[s4, src].astype(F32) + (b2r[0, c, loc].astype(F32) + b2r[1, c, loc].astype(F32)))
             hid = hid.astype(BF16)
             dst = pl.ds(mult(rows_of(chip) + t * BLOCK, BLOCK), BLOCK)
@@ -331,7 +358,7 @@
             def _():
                 own[c, loc] = hid
                 nxt = layer + 1
-                hbuf[c, dst] = normalise(hid.astype(F32), gain[nxt].astype(F32), bias[nxt].astype(F32)).astype(BF16)
+                hbuf[c, dst] = normalise(hid.astype(F32), gain[nxt], bias[nxt]).astype(BF16)
 
             @pl.when(layer + 1 >= n_layers)
             def _():
@@ -339,17 +366,18 @@
 
         for copy in copies_g1(u):
             copy.start()
-        for copy in copies_b1(u) + copies_b2(u):
-            copy.wait_send()
 
     def stage_g2(u):
-        first, second = copies_g1(u), copies_g2(u)
+        second = copies_g2(u)
         c = lax.rem(u, n_chunks)
-        same_rows(c, rows_of(chip_r), own_rows, g1_send.at[0, c], g1_recv.at[0, c], left).wait_recv()
+        from_r, from_l = rows_of(chip_r), rows_of(chip_l)
+        same_rows(c, mult(from_r + sub, sub), sub, g1_send.at[0, c], g1_recv.at[0, c], left).wait_recv()
         second[0].start()
+        same_rows(c, from_l, sub, g1_send.at[1, c], g1_recv.at[1, c], right).wait_recv()
+        second[1].start()
+        same_rows(c, from_r, sub, gn_send.at[0, c], gn_recv.at[0, c], left).wait_recv()
         second[2].start()
-        same_rows(c, rows_of(chip_l), own_rows, g1_send.at[1, c], g1_recv.at[1, c], right).wait_recv()
-        second[1].start()
+        same_rows(c, mult(from_l + sub, sub), sub, gn_send.at[1, c], gn_recv.at[1, c], right).wait_recv()
         second[3].start()
 
     def stage_g3(u):
@@ -358,6 +386,8 @@
         same_rows(c, mult(theirs + sub, sub), sub, g2_send.at[0, c], g2_recv.at[0, c], left).wait_recv()
         same_rows(c, theirs, sub, g2_send.at[1, c], g2_recv.at[1, c], right).wait_recv()
         copy_g3(u).start()
+        for copy in copies_b1(u) + copies_bd(u) + copies_b2(u):
+            copy.wait_send()
 
     def stage_g4(u):
         c = lax.rem(u, n_chunks)
@@ -376,28 +406,52 @@
         def _():
             stage(u)
 
-    own_copy.wait()
-    for c in range(n_chunks):
-        own[c] = xown[:, c * SEQS:(c + 1) * SEQS].astype(F32).reshape(own_rows, d_model).astype(BF16)
+    parts = {"qkv": piece_qkv, "mid": piece_mid, "out": piece_out, "b1": stage_b1, "b2": stage_b2, "b3": stage_b3,
+             "g2": stage_g2, "g3": stage_g3, "g4": stage_g4}
+
+    def greet():
+        pl.semaphore_wait(barrier, 3)
+
+    def fetch():
+        for layer in range(1, n_layers):
+            for copy in weight_copies(layer):
+                copy.start()
+        own_copy.wait()
+        for c in range(n_chunks):
+            own[c] = xown[:, c * SEQS:(c + 1) * SEQS].astype(F32).reshape(own_rows, d_model).astype(BF16)
 
     def tick(i, carry):
-        guarded(stage_g2, i - 4)
-        guarded(piece_qkv, i)
-        guarded(stage_b3, i - 3)
-        guarded(stage_g3, i - 5)
-        guarded(piece_attend, i)
-        guarded(stage_b2, i - 2)
-        guarded(stage_g4, i - 6)
-        guarded(piece_ff, i)
-        guarded(stage_b1, i - 1)
-        guarded(piece_out, i)
+        for name, lag in SCHEDULE:
+            guarded(parts[name], i - lag)
+            if name == "qkv":
+                pl.when(i == 0)(greet)
+                pl.when(i == 1)(fetch)
         return carry
 
-    lax.fori_loop(0, total + 6, tick, 0)
+    lax.fori_loop(0, total + max(lag for _, lag in SCHEDULE), tick, 0)
     for copy in kv_back(total - 1):
         copy.wait()
     for c in range(n_chunks):
         hid_copy(c).wait()
+
+
+def deliver(hid, k_new, v_new, hid_out, k_out, v_out, hid_buf, kv_buf, in_sem, out_sem):
+    n_chunks, _, seqs, _ = hid.shape
+    n_layers, batch = k_new.shape[:2]
+    size = kv_buf.shape[1]
+    moves = [(src.at[layer, pl.ds(b, size)], None, dst.at[layer, pl.ds(b, size)])
+             for src, dst in ((k_new, k_out), (v_new, v_out)) for layer in range(n_layers) for b in range(0, batch, size)]
+    moves = [(src, kv_buf.at[n], dst) for n, (src, _, dst) in enumerate(moves)]
+    moves += [(hid.at[c], hid_buf.at[c], hid_out.at[:, pl.ds(c * seqs, seqs), :]) for c in range(n_chunks)]
+    takes = [pltpu.make_async_copy(src, buf, in_sem.at[n]) for n, (src, buf, _) in enumerate(moves)]
+    gives = [pltpu.make_async_copy(buf, dst, out_sem.at[n]) for n, (_, buf, dst) in enumerate(moves)]
+    for copy in takes:
+        copy.start()
+    for take, give in zip(takes, gives):
+        take.wait()
+        give.start()
+    for copy in gives:
+        copy.wait()
 
 
 def decode_shard(x_steps, cur_len, k_cache, v_cache, ln_gain, ln_bias, w_q, w_k, w_v, w_o, w_in, b_in, w_out, b_out):
@@ -409,7 +463,6 @@
     width = heads * head_dim
     own_rows = rows // 8
     tab = rotary_table(128, head_dim)
-    cl_rows = jnp.broadcast_to(cur_len[:, None], (batch, 128))
     k_rows = k_cache.reshape(n_layers, batch, slots * heads, head_dim)
     v_rows = v_cache.reshape(n_layers, batch, slots * heads, head_dim)
     vmem = pl.BlockSpec(memory_space=pltpu.VMEM)
@@ -420,9 +473,13 @@
         functools.partial(kernel, dims),
         out_shape=(jax.ShapeDtypeStruct((n_chunks, rows, d_model), BF16),
                    jax.ShapeDtypeStruct(k_rows.shape, BF16), jax.ShapeDtypeStruct(v_rows.shape, BF16)),
-        in_specs=[pl.BlockSpec(memory_space=pltpu.SMEM)] + [vmem] * 6 + [hbm] * 9,
+        in_specs=[pl.BlockSpec(memory_space=pltpu.SMEM)] + [vmem] * 5 + [hbm] * 9,
         out_specs=(hbm, hbm, hbm),
         scratch_shapes=[
+            pltpu.VMEM((n_layers, 1, d_model), F32),
+            pltpu.VMEM((n_layers, 1, d_model), F32),
+            pltpu.VMEM((n_layers, 1, d_model), F32),
+            pltpu.VMEM((n_layers, 1, d_ff), F32),
             pltpu.VMEM((n_layers, d_model, 3 * width + d_ff), BF16),
             pltpu.VMEM((n_layers, width + d_ff, d_model), BF16),
             pltpu.VMEM((n_chunks, rows, d_model), BF16),
@@ -444,11 +501,24 @@
             dma((2,)), dma((4,)), dma((2, n_chunks)), dma((2, n_chunks)), dma((2, n_chunks)), dma((2, n_chunks)),
             dma((2, n_chunks)), dma((2, n_chunks)), dma((2, n_chunks)), dma((2, n_chunks)),
             dma((4, n_chunks)), dma((4, n_chunks)),
+            dma((2, n_chunks)), dma((2, n_chunks)), dma((2, n_chunks)), dma((2, n_chunks)),
         ],
         compiler_params=pltpu.CompilerParams(collective_id=0, has_side_effects=True, vmem_limit_bytes=67043328),
-    )(cur_len, cl_rows, tab, ln_gain[:, None, :], ln_bias[:, None, :], b_out[:, None, :], b_in[:, None, :], x_steps, k_rows, v_rows,
+    )(cur_len, tab, ln_gain, ln_bias, b_out, b_in, x_steps, k_rows, v_rows,
       w_q, w_k, w_v, w_in, w_o, w_out)
-    hidden = hid.reshape(n_chunks, steps, SEQS, d_model).transpose(1, 0, 2, 3).reshape(steps, batch, d_model)
+    size = 16
+    pieces = 2 * n_layers * batch // size
+    hidden, k_new, v_new = pl.pallas_call(
+        deliver,
+        out_shape=(jax.ShapeDtypeStruct(x_steps.shape, BF16),
+                   jax.ShapeDtypeStruct(k_rows.shape, BF16), jax.ShapeDtypeStruct(v_rows.shape, BF16)),
+        in_specs=[hbm] * 3,
+        out_specs=(hbm, hbm, hbm),
+        scratch_shapes=[pltpu.VMEM((n_chunks, steps, SEQS, d_model), BF16),
+                        pltpu.VMEM((pieces, size, slots * heads, head_dim), BF16),
+                        dma((pieces + n_chunks,)), dma((pieces + n_chunks,))],
+        compiler_params=pltpu.CompilerParams(vmem_limit_bytes=67043328),
+    )(hid.reshape(n_chunks, steps, SEQS, d_model), k_new, v_new)
     return hidden, k_new.reshape(k_cache.shape), v_new.reshape(v_cache.shape)
 
 

time: 260 us -> 183 us (0.70)
  Pallas kernels: 228 us -> 182 us
  local copies, waits for them, and re-layouts: 27 us -> 0 us
  other arithmetic: 4.05 us -> 0 us
    pallas_call x1, Pallas kernels: 228 us -> 164 us  [decode_shard(): pl.pallas_call(functools.partial(kernel, dims), out_shape=(jax.ShapeDtype...]
    pallas_call x0 -> x1, Pallas kernels: none -> 17.5 us  [decode_shard(): pl.pallas_call(deliver, out_shape=(jax.ShapeDtypeStruct(x_steps.shape, BF...]
    unnamed x6 -> x0, local copies, waits for them, and re-layouts: 11.6 us -> none
    reshape x3 -> x0, local copies, waits for them, and re-layouts: 8.78 us -> none  [the longest x1 8.59 us: decode_shard(): hid.reshape(n_chunks, steps, SEQS, d_model).transpose(1, 0, 2, 3)]
    broadcast_in_dim x6 -> x0, local copies, waits for them, and re-layouts: 6.59 us -> none  [the longest x1 1.35 us: decode_shard(): cl_rows = jnp.broadcast_to(cur_len[:, None], (batch, 128))]
    unnamed x6 -> x0, other arithmetic: 3.13 us -> none
where the time goes in v3:
time: 183 us
  Pallas kernels  182 us (99%)
    pallas_call x1, Pallas kernels, decode_shard(): pl.pallas_call(functools.partial(kernel, dims), out_shape=(jax.ShapeDtype...  164 us
    pallas_call x1, Pallas kernels, decode_shard(): pl.pallas_call(deliver, out_shape=(jax.ShapeDtypeStruct(x_steps.shape, BF...  17.5 us

profile of v3, /device:TPU:113, one launch (start us, length us, event | category | flops | bytes accessed | tf_op | source)
XLA Modules:
  0.0 182.5 jit_solution(3872080349189197954)
XLA Ops:
  0.6 164.3 %shard_map.166 = (bf16[8,256,2048]{2,1,0:T(8,128)(2,1)}, bf16[2,64,256,128]{3,2,1,0:T(8,128)(2,1)}, bf16[2,64,256,128]{3,2,1,0:T(8,128)(2,1)}) custom-call(s32[64]{0:T(128)} %cl_s.1, bf16[128,768]{1,0:T(8,128)(2,1)} %constant.2.clone.tab, bf16[2,2048]{1,0:T(2,128)(2,1)} %gain_in.1, bf16[2,2048]{1,0:T(2,128)(2,1)} %bias_in.1, bf16[2,2048]{1,0:T(2,128)(2,1)} %bout_in.1, ...), custom_call_target="tpu_custom_call" | custom-call | tf_op jit(solution)/shard_map/pallas_call | solution.py:472
  165.0 17.5 %shard_map.167 = (bf16[32,64,2048]{2,1,0:T(8,128)(2,1)}, bf16[2,64,256,128]{3,2,1,0:T(8,128)(2,1)}, bf16[2,64,256,128]{3,2,1,0:T(8,128)(2,1)}) custom-call(bf16[8,32,8,2048]{3,2,1,0:T(8,128)(2,1)} %bitcast.5, bf16[2,64,256,128]{3,2,1,0:T(8,128)(2,1)} %get-tuple-element.10.k_new, bf16[2,64,256,128]{3,2,1,0:T(8,128)(2,1)} %get-tuple-element.11.v_new), custom_call_target="tpu_custom_call" | custom-call | tf_op jit(solution)/shard_map/pallas_call | solution.py:511

commit v4 on v3

--- a/solution.py
+++ b/solution.py
@@ -44,9 +44,9 @@
 
 
 def kernel(dims, cl_s, tab, gain_in, bias_in, bout_in, bin_in, x_hbm, k_hbm, v_hbm, wq, wk, wv, win, wo, wout,
-           hid_out, k_out, v_out,
-           gain, bias, bout, bin_, w1, w2, hbuf, own, xown, xbuf, kbuf, vbuf, qkv, cs, ctx, mid, part, arecv, pair, b1r, b2r,
-           w_sem, x_sem, xo_sem, kv_sem, kvo_sem, out_sem,
+           hbuf, k_out, v_out,
+           gain, bias, bout, bin_, w1, w2, own, xown, xbuf, kbuf, vbuf, qkv, cs, ctx, mid, part, arecv, pair, b1r, b2r,
+           w_sem, x_sem, xo_sem, kv_sem,
            a_send, a_recv, b1_send, b1_recv, b2_send, b2_recv, g1_send, g1_recv, g2_send, g2_recv, d_send, d_recv,
            bd_send, bd_recv, gn_send, gn_recv):
     n_layers, n_chunks, steps, heads, head_dim, d_model, d_ff = dims
@@ -80,12 +80,12 @@
         pl.semaphore_signal(barrier, inc=1, device_id={"tp": dev}, device_id_type=MESH)
 
     def weight_copies(layer):
-        return [pltpu.make_async_copy(wq.at[layer], w1.at[layer, :, pl.ds(0, width)], w_sem.at[layer, 0]),
-                pltpu.make_async_copy(wk.at[layer], w1.at[layer, :, pl.ds(width, width)], w_sem.at[layer, 1]),
-                pltpu.make_async_copy(wv.at[layer], w1.at[layer, :, pl.ds(2 * width, width)], w_sem.at[layer, 2]),
-                pltpu.make_async_copy(win.at[layer], w1.at[layer, :, pl.ds(3 * width, d_ff)], w_sem.at[layer, 3]),
-                pltpu.make_async_copy(wo.at[layer], w2.at[layer, pl.ds(0, width), :], w_sem.at[layer, 4]),
-                pltpu.make_async_copy(wout.at[layer], w2.at[layer, pl.ds(width, d_ff), :], w_sem.at[layer, 5])]
+        return [pltpu.make_async_copy(wq.at[layer], w1.at[:, pl.ds(0, width)], w_sem.at[0]),
+                pltpu.make_async_copy(wk.at[layer], w1.at[:, pl.ds(width, width)], w_sem.at[1]),
+                pltpu.make_async_copy(wv.at[layer], w1.at[:, pl.ds(2 * width, width)], w_sem.at[2]),
+                pltpu.make_async_copy(win.at[layer], w1.at[:, pl.ds(3 * width, d_ff)], w_sem.at[3]),
+                pltpu.make_async_copy(wo.at[layer], w2.at[pl.ds(0, width), :], w_sem.at[4]),
+                pltpu.make_async_copy(wout.at[layer], w2.at[pl.ds(width, d_ff), :], w_sem.at[5])]
 
     def x_copy(c):
         return pltpu.make_async_copy(x_hbm.at[:, pl.ds(mult(c * SEQS, SEQS), SEQS), :], xbuf.at[lax.rem(c, 2)],
@@ -96,15 +96,6 @@
         seqs = pl.ds(mult(c * SEQS, SEQS), SEQS)
         return [pltpu.make_async_copy(k_hbm.at[layer, seqs], kbuf.at[s], kv_sem.at[0, s]),
                 pltpu.make_async_copy(v_hbm.at[layer, seqs], vbuf.at[s], kv_sem.at[1, s])]
-
-    def kv_back(i):
-        layer, c, s = lax.div(i, n_chunks), lax.rem(i, n_chunks), lax.rem(i, 2)
-        seqs = pl.ds(mult(c * SEQS, SEQS), SEQS)
-        return [pltpu.make_async_copy(kbuf.at[s], k_out.at[layer, seqs], kvo_sem.at[0, s]),
-                pltpu.make_async_copy(vbuf.at[s], v_out.at[layer, seqs], kvo_sem.at[1, s])]
-
-    def hid_copy(c):
-        return pltpu.make_async_copy(hbuf.at[c], hid_out.at[c], out_sem.at[c])
 
     steps_own = own_rows // SEQS
     own_copy = pltpu.make_async_copy(x_hbm.at[pl.ds((core * 4 + chip) * steps_own, steps_own)], xown, xo_sem)
@@ -121,13 +112,20 @@
         for dst, src in ((gain, gain_in), (bias, bias_in), (bout, bout_in), (bin_, bin_in)):
             dst[layer] = src[layer:layer + 1].astype(F32)
 
+    def take_weights(i, lo, hi):
+        @pl.when(lax.rem(i, n_chunks) == 0)
+        def _():
+            for copy in weight_copies(lax.div(i, n_chunks))[lo:hi]:
+                copy.wait()
+
+    def next_weights(i, lo, hi):
+        @pl.when((lax.rem(i, n_chunks) == n_chunks - 1) & (i + 1 < total))
+        def _():
+            for copy in weight_copies(lax.div(i, n_chunks) + 1)[lo:hi]:
+                copy.start()
+
     def piece_qkv(i):
         layer, c = lax.div(i, n_chunks), lax.rem(i, n_chunks)
-
-        @pl.when(i >= 1)
-        def _():
-            for copy in kv_back(i - 1):
-                copy.wait()
 
         @pl.when(i + 1 < total)
         def _():
@@ -152,11 +150,7 @@
 
             lax.fori_loop(0, rows // BLOCK, block, 0, unroll=8)
 
-        for layer_w in range(n_layers):
-            @pl.when(i == layer_w * n_chunks)
-            def _(layer_w=layer_w):
-                for copy in weight_copies(layer_w)[:3]:
-                    copy.wait()
+        take_weights(i, 0, 3)
 
         row = lax.broadcasted_iota(jnp.int32, (rows, 128), 0)
         pos = lax.div(row, SEQS)
@@ -168,24 +162,22 @@
         cs[:, 0:e] = (tabs[:, 0:e] + tabs[:, e:2 * e]) + tabs[:, 2 * e:3 * e]
         cs[:, e:2 * e] = (tabs[:, 3 * e:4 * e] + tabs[:, 4 * e:5 * e]) + tabs[:, 5 * e:6 * e]
         even = lax.rem(lax.broadcasted_iota(jnp.int32, (rows, e), 1), 2) == 0
-        qk = jnp.dot(hbuf[c], w1[layer, :, pl.ds(0, 2 * width)], preferred_element_type=F32)
+        qk = jnp.dot(hbuf[c], w1[:, pl.ds(0, 2 * width)], preferred_element_type=F32)
         for h in range(2 * heads):
             vec = qk[:, h * e:(h + 1) * e]
             other = jnp.where(even, pltpu.roll(vec, e - 1, 1), pltpu.roll(vec, 1, 1))
             qkv[h] = vec * cs[:, 0:e] + other * cs[:, e:2 * e]
-        val = jnp.dot(hbuf[c], w1[layer, :, pl.ds(2 * width, width)], preferred_element_type=F32)
+        val = jnp.dot(hbuf[c], w1[:, pl.ds(2 * width, width)], preferred_element_type=F32)
         for h in range(heads):
             qkv[2 * heads + h] = val[:, h * e:(h + 1) * e]
+        next_weights(i, 0, 3)
 
     def piece_mid(i):
-        for layer_w in range(n_layers):
-            @pl.when(i == layer_w * n_chunks)
-            def _(layer_w=layer_w):
-                for copy in weight_copies(layer_w)[3:]:
-                    copy.wait()
+        take_weights(i, 3, 6)
 
         piece_ff(i)
         piece_attend(i)
+        next_weights(i, 3, 4)
 
     def piece_attend(i):
         layer, c, s = lax.div(i, n_chunks), lax.rem(i, n_chunks), lax.rem(i, 2)
@@ -218,8 +210,8 @@
             scores = [lax.dot_general(q, k, (((1,), (1,)), ((), ())), preferred_element_type=F32) * scale
                       for q, k in zip(queries, k_all)]
             for b, k, v in zip(group, k_all, v_all):
-                kbuf[s, b] = k
-                vbuf[s, b] = v
+                k_out[layer, c * SEQS + b] = k
+                v_out[layer, c * SEQS + b] = v
             scores = [jnp.where(seen <= n, sc, -jnp.inf) for sc, n in zip(scores, lens)]
             exps = [jnp.exp(sc - jnp.max(sc, axis=-1, keepdims=True)) for sc in scores]
             probs = [(ex / jnp.sum(ex, axis=-1, keepdims=True)).astype(BF16) for ex in exps]
@@ -229,8 +221,6 @@
                     ctx[h, pl.ds(b, steps, stride=SEQS), :] = context[h * steps:(h + 1) * steps]
         for h in range(heads):
             mid[:, h * e:(h + 1) * e] = ctx[h].astype(BF16)
-        for copy in kv_back(i):
-            copy.start()
 
     def piece_ff(i):
         layer, c = lax.div(i, n_chunks), lax.rem(i, n_chunks)
@@ -238,7 +228,7 @@
 
         def block(j, carry):
             cols = mult(j * tile, tile)
-            pre = jnp.dot(hbuf[c], w1[layer, :, pl.ds(mult(3 * width + cols, 256), tile)], preferred_element_type=F32)
+            pre = jnp.dot(hbuf[c], w1[:, pl.ds(mult(3 * width + cols, 256), tile)], preferred_element_type=F32)
             pre = pre + bin_[layer, :, pl.ds(cols, tile)]
             inner = 0.7978845608028654 * (pre + 0.044715 * (pre * pre * pre))
             mid[:, pl.ds(mult(width + cols, 256), tile)] = (pre * (0.5 * (1.0 + jnp.tanh(inner)))).astype(BF16)
@@ -252,11 +242,12 @@
 
         def block(j, carry):
             cols = pl.ds(mult(j * tile, tile), tile)
-            part[s, :, cols] = jnp.dot(mid[...], w2[layer, :, cols], preferred_element_type=F32).astype(BF16)
+            part[s, :, cols] = jnp.dot(mid[...], w2[:, cols], preferred_element_type=F32).astype(BF16)
             return carry
 
         lax.fori_loop(0, d_model // tile, block, 0, unroll=True)
         copy_a(i).start()
+        next_weights(i, 4, 6)
 
     def copy_a(u):
         s2, s4 = lax.rem(u, 2), lax.rem(u, 4)
@@ -397,10 +388,6 @@
         for copy in copies_g1(u) + copies_g2(u) + [copy_g3(u)]:
             copy.wait_send()
 
-        @pl.when(u >= total - n_chunks)
-        def _():
-            hid_copy(c).start()
-
     def guarded(stage, u):
         @pl.when((u >= 0) & (u < total))
         def _():
@@ -413,9 +400,6 @@
         pl.semaphore_wait(barrier, 3)
 
     def fetch():
-        for layer in range(1, n_layers):
-            for copy in weight_copies(layer):
-                copy.start()
         own_copy.wait()
         for c in range(n_chunks):
             own[c] = xown[:, c * SEQS:(c + 1) * SEQS].astype(F32).reshape(own_rows, d_model).astype(BF16)
@@ -429,28 +413,22 @@
         return carry
 
     lax.fori_loop(0, total + max(lag for _, lag in SCHEDULE), tick, 0)
-    for copy in kv_back(total - 1):
-        copy.wait()
-    for c in range(n_chunks):
-        hid_copy(c).wait()
-
-
-def deliver(hid, k_new, v_new, hid_out, k_out, v_out, hid_buf, kv_buf, in_sem, out_sem):
-    n_chunks, _, seqs, _ = hid.shape
-    n_layers, batch = k_new.shape[:2]
-    size = kv_buf.shape[1]
-    moves = [(src.at[layer, pl.ds(b, size)], None, dst.at[layer, pl.ds(b, size)])
-             for src, dst in ((k_new, k_out), (v_new, v_out)) for layer in range(n_layers) for b in range(0, batch, size)]
-    moves = [(src, kv_buf.at[n], dst) for n, (src, _, dst) in enumerate(moves)]
-    moves += [(hid.at[c], hid_buf.at[c], hid_out.at[:, pl.ds(c * seqs, seqs), :]) for c in range(n_chunks)]
-    takes = [pltpu.make_async_copy(src, buf, in_sem.at[n]) for n, (src, buf, _) in enumerate(moves)]
-    gives = [pltpu.make_async_copy(buf, dst, out_sem.at[n]) for n, (_, buf, dst) in enumerate(moves)]
-    for copy in takes:
+
+
+def deliver(hid, k_new, v_new, hid_out, k_out, v_out, out_sem):
+    n_chunks, rows, d_model = hid.shape
+    steps = hid_out.shape[0]
+    seqs = rows // steps
+    moves = [(hid.at[c].reshape(steps, seqs, d_model), hid_out.at[:, pl.ds(c * seqs, seqs), :]) for c in range(n_chunks)]
+    for src, dst in ((k_new, k_out), (v_new, v_out)):
+        n_layers, batch = src.shape[:2]
+        size = batch // 4
+        moves += [(src.at[layer, pl.ds(b, size)], dst.at[layer, pl.ds(b, size)])
+                  for layer in range(n_layers) for b in range(0, batch, size)]
+    copies = [pltpu.make_async_copy(src, dst, out_sem.at[n]) for n, (src, dst) in enumerate(moves)]
+    for copy in copies:
         copy.start()
-    for take, give in zip(takes, gives):
-        take.wait()
-        give.start()
-    for copy in gives:
+    for copy in copies:
         copy.wait()
 
 
@@ -471,18 +449,16 @@
     dma = pltpu.SemaphoreType.DMA
     hid, k_new, v_new = pl.pallas_call(
         functools.partial(kernel, dims),
-        out_shape=(jax.ShapeDtypeStruct((n_chunks, rows, d_model), BF16),
-                   jax.ShapeDtypeStruct(k_rows.shape, BF16), jax.ShapeDtypeStruct(v_rows.shape, BF16)),
+        out_shape=(pltpu.VMEM((n_chunks, rows, d_model), BF16), pltpu.VMEM(k_rows.shape, BF16), pltpu.VMEM(v_rows.shape, BF16)),
         in_specs=[pl.BlockSpec(memory_space=pltpu.SMEM)] + [vmem] * 5 + [hbm] * 9,
-        out_specs=(hbm, hbm, hbm),
+        out_specs=(vmem, vmem, vmem),
         scratch_shapes=[
             pltpu.VMEM((n_layers, 1, d_model), F32),
             pltpu.VMEM((n_layers, 1, d_model), F32),
             pltpu.VMEM((n_layers, 1, d_model), F32),
             pltpu.VMEM((n_layers, 1, d_ff), F32),
-            pltpu.VMEM((n_layers, d_model, 3 * width + d_ff), BF16),
-            pltpu.VMEM((n_layers, width + d_ff, d_model), BF16),
-            pltpu.VMEM((n_chunks, rows, d_model), BF16),
+            pltpu.VMEM((d_model, 3 * width + d_ff), BF16),
+            pltpu.VMEM((width + d_ff, d_model), BF16),
             pltpu.VMEM((n_chunks, own_rows, d_model), BF16),
             pltpu.VMEM((own_rows // SEQS, batch, d_model), BF16),
             pltpu.VMEM((2, steps, SEQS, d_model), BF16),
@@ -497,28 +473,24 @@
             pltpu.VMEM((4, rows // 2, d_model), BF16),
             pltpu.VMEM((2, n_chunks, own_rows // 2, d_model), BF16),
             pltpu.VMEM((2, n_chunks, own_rows, d_model), BF16),
-            dma((n_layers, 6)), dma((2,)), dma, dma((2, 2)), dma((2, 2)), dma((n_chunks,)),
+            dma((6,)), dma((2,)), dma, dma((2, 2)),
             dma((2,)), dma((4,)), dma((2, n_chunks)), dma((2, n_chunks)), dma((2, n_chunks)), dma((2, n_chunks)),
             dma((2, n_chunks)), dma((2, n_chunks)), dma((2, n_chunks)), dma((2, n_chunks)),
             dma((4, n_chunks)), dma((4, n_chunks)),
             dma((2, n_chunks)), dma((2, n_chunks)), dma((2, n_chunks)), dma((2, n_chunks)),
         ],
-        compiler_params=pltpu.CompilerParams(collective_id=0, has_side_effects=True, vmem_limit_bytes=67043328),
+        compiler_params=pltpu.CompilerParams(collective_id=0, has_side_effects=True, vmem_limit_bytes=38 * 2**20),
     )(cur_len, tab, ln_gain, ln_bias, b_out, b_in, x_steps, k_rows, v_rows,
       w_q, w_k, w_v, w_in, w_o, w_out)
-    size = 16
-    pieces = 2 * n_layers * batch // size
     hidden, k_new, v_new = pl.pallas_call(
         deliver,
         out_shape=(jax.ShapeDtypeStruct(x_steps.shape, BF16),
                    jax.ShapeDtypeStruct(k_rows.shape, BF16), jax.ShapeDtypeStruct(v_rows.shape, BF16)),
-        in_specs=[hbm] * 3,
+        in_specs=[vmem] * 3,
         out_specs=(hbm, hbm, hbm),
-        scratch_shapes=[pltpu.VMEM((n_chunks, steps, SEQS, d_model), BF16),
-                        pltpu.VMEM((pieces, size, slots * heads, head_dim), BF16),
-                        dma((pieces + n_chunks,)), dma((pieces + n_chunks,))],
-        compiler_params=pltpu.CompilerParams(vmem_limit_bytes=67043328),
-    )(hid.reshape(n_chunks, steps, SEQS, d_model), k_new, v_new)
+        scratch_shapes=[dma((n_chunks + 8 * n_layers,))],
+        compiler_params=pltpu.CompilerParams(vmem_limit_bytes=2**20),
+    )(*[pltpu.with_memory_space_constraint(a, pltpu.VMEM) for a in (hid, k_new, v_new)])
     return hidden, k_new.reshape(k_cache.shape), v_new.reshape(v_cache.shape)
 
 

time: 183 us -> 172 us (0.940)
  Pallas kernels: 182 us -> 171 us
    pallas_call x1, Pallas kernels: 17.5 us -> 8.56 us  [decode_shard(): pl.pallas_call(deliver, out_shape=(jax.ShapeDtypeStruct(x_steps.shape, BF...]
where the time goes in v4:
time: 172 us
  Pallas kernels  171 us (99%)
    pallas_call x1, Pallas kernels, decode_shard(): pl.pallas_call(functools.partial(kernel, dims), out_shape=(pltpu.VMEM((n_...  163 us
    pallas_call x1, Pallas kernels, decode_shard(): pl.pallas_call(deliver, out_shape=(jax.ShapeDtypeStruct(x_steps.shape, BF...  8.56 us

profile of v4, /device:TPU:113, one launch (start us, length us, event | category | flops | bytes accessed | tf_op | source)
XLA Modules:
  0.0 172.0 jit_solution(12575299440519186619)
XLA Ops:
  0.6 162.8 %shard_map.166 = (bf16[8,256,2048]{2,1,0:T(8,128)(2,1)S(1)}, bf16[2,64,256,128]{3,2,1,0:T(8,128)(2,1)S(1)}, bf16[2,64,256,128]{3,2,1,0:T(8,128)(2,1)S(1)}) custom-call(s32[64]{0:T(128)} %cl_s.1, bf16[128,768]{1,0:T(8,128)(2,1)} %constant.2.clone.tab, bf16[2,2048]{1,0:T(2,128)(2,1)} %gain_in.1, bf16[2,2048]{1,0:T(2,128)(2,1)} %bias_in.1, ...), custom_call_target="tpu_custom_call" | custom-call | tf_op jit(solution)/shard_map/pallas_call | solution.py:450
  163.5 8.6 %shard_map.167 = (bf16[32,64,2048]{2,1,0:T(8,128)(2,1)}, bf16[2,64,256,128]{3,2,1,0:T(8,128)(2,1)}, bf16[2,64,256,128]{3,2,1,0:T(8,128)(2,1)}) custom-call(bf16[8,256,2048]{2,1,0:T(8,128)(2,1)S(1)} %get-tuple-element.9.hid, bf16[2,64,256,128]{3,2,1,0:T(8,128)(2,1)S(1)} %get-tuple-element.10.k_new, bf16[2,64,256,128]{3,2,1,0:T(8,128)(2,1)S(1)} %get-tuple-element.11.v_new), custom_call_target="tpu_custom_call" | custom-call | tf_op jit(solution)/shard_map/pallas_call | solution.py:485

commit v5 on v4

--- a/solution.py
+++ b/solution.py
@@ -13,7 +13,7 @@
 SEQS = 8
 GROUP = 8
 BLOCK = 16
-SCHEDULE = (("qkv", 0), ("b1", 1), ("g2", 3), ("g4", 4), ("mid", 0), ("b3", 2), ("out", 0), ("b2", 1), ("g3", 3))
+SCHEDULE = (("qkv", 0), ("b1", 1), ("g3", 4), ("mid", 0), ("att", 0), ("g2", 3), ("b3", 2), ("out", 0), ("b2", 1), ("g4", 4))
 MESH = pl.DeviceIdType.MESH
 F32 = jnp.float32
 BF16 = jnp.bfloat16
@@ -162,12 +162,12 @@
         cs[:, 0:e] = (tabs[:, 0:e] + tabs[:, e:2 * e]) + tabs[:, 2 * e:3 * e]
         cs[:, e:2 * e] = (tabs[:, 3 * e:4 * e] + tabs[:, 4 * e:5 * e]) + tabs[:, 5 * e:6 * e]
         even = lax.rem(lax.broadcasted_iota(jnp.int32, (rows, e), 1), 2) == 0
-        qk = jnp.dot(hbuf[c], w1[:, pl.ds(0, 2 * width)], preferred_element_type=F32)
+        qk = jnp.dot(hbuf[c], w1[:, pl.ds(0, 3 * width)], preferred_element_type=F32)
         for h in range(2 * heads):
             vec = qk[:, h * e:(h + 1) * e]
             other = jnp.where(even, pltpu.roll(vec, e - 1, 1), pltpu.roll(vec, 1, 1))
             qkv[h] = vec * cs[:, 0:e] + other * cs[:, e:2 * e]
-        val = jnp.dot(hbuf[c], w1[:, pl.ds(2 * width, width)], preferred_element_type=F32)
+        val = qk[:, 2 * width:3 * width]
         for h in range(heads):
             qkv[2 * heads + h] = val[:, h * e:(h + 1) * e]
         next_weights(i, 0, 3)
@@ -176,7 +176,6 @@
         take_weights(i, 3, 6)
 
         piece_ff(i)
-        piece_attend(i)
         next_weights(i, 3, 4)
 
     def piece_attend(i):
@@ -224,7 +223,7 @@
 
     def piece_ff(i):
         layer, c = lax.div(i, n_chunks), lax.rem(i, n_chunks)
-        tile = 512
+        tile = 1024
 
         def block(j, carry):
             cols = mult(j * tile, tile)
@@ -238,7 +237,7 @@
 
     def piece_out(i):
         layer, s = lax.div(i, n_chunks), lax.rem(i, 2)
-        tile = 512
+        tile = 1024
 
         def block(j, carry):
             cols = pl.ds(mult(j * tile, tile), tile)
@@ -393,7 +392,7 @@
         def _():
             stage(u)
 
-    parts = {"qkv": piece_qkv, "mid": piece_mid, "out": piece_out, "b1": stage_b1, "b2": stage_b2, "b3": stage_b3,
+    parts = {"qkv": piece_qkv, "mid": piece_mid, "att": piece_attend, "out": piece_out, "b1": stage_b1, "b2": stage_b2, "b3": stage_b3,
              "g2": stage_g2, "g3": stage_g3, "g4": stage_g4}
 
     def greet():
@@ -409,6 +408,7 @@
             guarded(parts[name], i - lag)
             if name == "qkv":
                 pl.when(i == 0)(greet)
+            if name == "mid":
                 pl.when(i == 1)(fetch)
         return carry
 

time: 172 us -> 172 us (level)
  no operation moved by 1% of the time
where the time goes in v5:
time: 172 us
  Pallas kernels  171 us (99%)
    pallas_call x1, Pallas kernels, decode_shard(): pl.pallas_call(functools.partial(kernel, dims), out_shape=(pltpu.VMEM((n_...  163 us
    pallas_call x1, Pallas kernels, decode_shard(): pl.pallas_call(deliver, out_shape=(jax.ShapeDtypeStruct(x_steps.shape, BF...  8.56 us

profile of v5, /device:TPU:113, one launch (start us, length us, event | category | flops | bytes accessed | tf_op | source)
XLA Modules:
  0.0 171.7 jit_solution(12833028486885360233)
XLA Ops:
  0.6 162.5 %shard_map.166 = (bf16[8,256,2048]{2,1,0:T(8,128)(2,1)S(1)}, bf16[2,64,256,128]{3,2,1,0:T(8,128)(2,1)S(1)}, bf16[2,64,256,128]{3,2,1,0:T(8,128)(2,1)S(1)}) custom-call(s32[64]{0:T(128)} %cl_s.1, bf16[128,768]{1,0:T(8,128)(2,1)} %constant.2.clone.tab, bf16[2,2048]{1,0:T(2,128)(2,1)} %gain_in.1, bf16[2,2048]{1,0:T(2,128)(2,1)} %bias_in.1, ...), custom_call_target="tpu_custom_call" | custom-call | tf_op jit(solution)/shard_map/pallas_call | solution.py:450
  163.1 8.6 %shard_map.167 = (bf16[32,64,2048]{2,1,0:T(8,128)(2,1)}, bf16[2,64,256,128]{3,2,1,0:T(8,128)(2,1)}, bf16[2,64,256,128]{3,2,1,0:T(8,128)(2,1)}) custom-call(bf16[8,256,2048]{2,1,0:T(8,128)(2,1)S(1)} %get-tuple-element.9.hid, bf16[2,64,256,128]{3,2,1,0:T(8,128)(2,1)S(1)} %get-tuple-element.10.k_new, bf16[2,64,256,128]{3,2,1,0:T(8,128)(2,1)S(1)} %get-tuple-element.11.v_new), custom_call_target="tpu_custom_call" | custom-call | tf_op jit(solution)/shard_map/pallas_call | solution.py:485
